TPU v7x, 32 devices: a whole 2x2x4 slice. The times are simulated.
32 devices in a mesh: gx: 2 (over core), gy: 4 (over y, x), gz: 4 (over z).
Axes of the slice: x: 2, y: 2, z: 4, core: 2. Of those that a mesh axis runs over, the one named last changes fastest.
Arguments:
- block_values: bfloat16 [4, 64, 4, 6, 128, 128], P('gy', 'gx', 'gz'), as said below
- block_cols: int32 [4, 64, 4, 6], P('gy', 'gx', 'gz'), may hold values from 0 to 63, as said below
Outputs:
- purified: float32 [256, 32768], P(('gx', 'gy'), 'gz')
Inputs may be any that keep to these rules, and one draw needn't show every extreme that they name: block_cols[a, s, b, :] holds 6 distinct tile columns of panel b at which tile row a * 64 + s of P is nonzero; every tile column of a panel is listed by exactly 6 tile rows of each slab; the pattern is symmetric: tile (i, j) is listed exactly when tile (j, i) is. `block_values`: P is symmetric: the tile listed at (i, j) is the transpose of the tile listed at (j, i), and diagonal tiles are symmetric.
All inputs are finite; a program needn't handle non-finite values.
Results may differ from a plain program's by a relative error of at most 0.0033.
Values may be sent and summed in bfloat16 or wider, within the bound.
A program may use at most 128 MiB of HBM per device.

v0:
```python
import functools

import jax
import jax.numpy as jnp
from jax import lax
from jax.experimental import pallas as pl
from jax.experimental.pallas import tpu as pltpu
from jax.sharding import PartitionSpec as P

WIN = 1
LANES = 128
MESH = pl.DeviceIdType.MESH


def pieces_of(count, most):
    for pieces in range(min(count, most), 0, -1):
        if count % pieces == 0:
            return pieces


def greet(axes):
    barrier = pltpu.get_barrier_semaphore()
    total = 0
    for axis in axes:
        size = lax.axis_size(axis)
        me = lax.axis_index(axis)
        for step in range(1, size):
            pl.semaphore_signal(
                barrier, inc=1, device_id={axis: lax.rem(me + step, size)}, device_id_type=MESH
            )
        total += size - 1
    pl.semaphore_wait(barrier, total)


def remote(src, dst, send, recv, axis, peer):
    return pltpu.make_async_remote_copy(
        src_ref=src, dst_ref=dst, send_sem=send, recv_sem=recv,
        device_id={axis: peer}, device_id_type=MESH,
    )


def gather_kernel(
    n_gx, n_gy, pieces, tiles, cols, panel, panel_cols, left, left_cols,
    stage, load_sem, own_sem, send_sem, recv_sem, col_own, col_send, col_recv,
    win_own, win_send, win_recv,
):
    gx, gy = lax.axis_index("gx"), lax.axis_index("gy")
    rows = tiles.shape[0]
    part = rows // pieces
    loads = []
    for p in range(pieces):
        span = pl.ds(p * part, part)
        loads.append(pltpu.make_async_copy(tiles.at[span], stage.at[span], load_sem.at[p]))
        loads[-1].start()
    greet(("gx", "gy"))
    window = stage.at[pl.ds(0, WIN)]
    col_copies = [pltpu.make_async_copy(cols, panel_cols.at[gx], col_own)]
    for step in range(1, n_gx):
        col_copies.append(
            remote(cols, panel_cols.at[gx], col_send.at[step], col_recv.at[step],
                   "gx", lax.rem(gx + step, n_gx))
        )
    for copy in col_copies:
        copy.start()
    copies = []
    for p in range(pieces):
        loads[p].wait()
        if p == 0:
            @pl.when(gy == 0)
            def _():
                for peer in range(1, n_gy):
                    remote(window, left, win_send.at[0, peer], win_recv.at[0], "gy", peer).start()
                    remote(cols, left_cols, win_send.at[1, peer], win_recv.at[1], "gy", peer).start()
                pltpu.make_async_copy(window, left, win_own.at[0]).start()
                pltpu.make_async_copy(cols, left_cols, win_own.at[1]).start()
        source = stage.at[pl.ds(p * part, part)]
        target = panel.at[pl.ds(gx * rows + p * part, part)]
        for step in range(1, n_gx):
            copy = remote(source, target, send_sem.at[step, p], recv_sem.at[step, p],
                          "gx", lax.rem(gx + step, n_gx))
            copy.start()
            copies.append(copy)
        copy = pltpu.make_async_copy(source, target, own_sem.at[p])
        copy.start()
        copies.append(copy)
    for copy in col_copies + copies:
        copy.wait()

    @pl.when(gy == 0)
    def _():
        for peer in range(1, n_gy):
            remote(window, left, win_send.at[0, peer], win_recv.at[0], "gy", peer).wait_send()
            remote(cols, left_cols, win_send.at[1, peer], win_recv.at[1], "gy", peer).wait_send()
        pltpu.make_async_copy(window, left, win_own.at[0]).wait()
        pltpu.make_async_copy(cols, left_cols, win_own.at[1]).wait()

    @pl.when(gy != 0)
    def _():
        remote(window, left, win_send.at[0, 0], win_recv.at[0], "gy", 0).wait_recv()
        remote(cols, left_cols, win_send.at[1, 0], win_recv.at[1], "gy", 0).wait_recv()


def gather(tiles, cols):
    n_gx, n_gy = lax.axis_size("gx"), lax.axis_size("gy")
    rows = tiles.shape[0]
    pieces = pieces_of(rows, 4)
    padded = jnp.pad(cols, ((0, 0), (0, LANES - cols.shape[1])))
    dma = pltpu.SemaphoreType.DMA
    return pl.pallas_call(
        functools.partial(gather_kernel, n_gx, n_gy, pieces),
        out_shape=(
            jax.ShapeDtypeStruct((n_gx * rows,) + tiles.shape[1:], tiles.dtype),
            jax.ShapeDtypeStruct((n_gx,) + padded.shape, padded.dtype),
            jax.ShapeDtypeStruct((WIN,) + tiles.shape[1:], tiles.dtype),
            jax.ShapeDtypeStruct(padded.shape, padded.dtype),
        ),
        in_specs=[
            pl.BlockSpec(memory_space=pl.ANY),
            pl.BlockSpec(memory_space=pltpu.VMEM),
        ],
        out_specs=[pl.BlockSpec(memory_space=pl.ANY)] * 4,
        scratch_shapes=[
            pltpu.VMEM(tiles.shape, tiles.dtype),
            dma((pieces,)), dma((pieces,)), dma((n_gx, pieces)), dma((n_gx, pieces)),
            dma, dma((n_gx,)), dma((n_gx,)),
            dma((2,)), dma((2, n_gy)), dma((2,)),
        ],
        compiler_params=pltpu.CompilerParams(collective_id=0, has_side_effects=True),
        name="gather_tiles",
    )(tiles, padded)


def first_kernel(
    slots, pairs, left_cols, panel_cols, left, panel, out, rows_out,
    inverse, place, which, stage, sem,
):
    groups, height = out.shape[0], out.shape[2]

    for c in range(inverse.shape[0]):
        inverse[c] = -1
    for c in range(pairs, rows_out.shape[1]):
        rows_out[0, c] = 0
    for k in range(slots):
        inverse[left_cols[0, k]] = k
    entries = panel.shape[0]
    group = pieces_of(entries, 32)

    def scan(step, found):
        base = step * group
        matches = [inverse[panel_cols[base + j]] for j in range(group)]
        for j, k in enumerate(matches):
            place[found] = base + j
            which[found] = k
            found = found + (k >= 0).astype(jnp.int32)
        return found

    lax.fori_loop(0, entries // group, scan, jnp.int32(0))
    bunch = pairs // pieces_of(pairs, 4)
    copies = []
    for n in range(pairs):
        copies.append(pltpu.make_async_copy(panel.at[place[n]], stage.at[n], sem.at[n]))
        copies[-1].start()
    for n in range(pairs):
        rows_out[0, n] = lax.div(place[n], jnp.int32(slots))
    for first_pair in range(0, pairs, bunch):
        span = range(first_pair, first_pair + bunch)
        for n in span:
            copies[n].wait()
        for n in span:
            product = lax.dot_general(
                left[which[n]], stage[n], (((1,), (1,)), ((), ())),
                preferred_element_type=jnp.float32,
            ).astype(out.dtype)
            for g in range(groups):
                out[g, n] = product[g * height:(g + 1) * height]


def first(left, left_cols, panel, panel_cols):
    count, slots, size = panel.shape[0], panel.shape[1], panel.shape[2]
    pairs = slots * slots
    groups = lax.axis_size("gz")
    smem = pl.BlockSpec(memory_space=pltpu.SMEM)
    vmem = pl.BlockSpec(memory_space=pltpu.VMEM)
    return pl.pallas_call(
        functools.partial(first_kernel, slots, pairs),
        out_shape=(
            jax.ShapeDtypeStruct((groups, pairs, size // groups, size), panel.dtype),
            jax.ShapeDtypeStruct((1, LANES), jnp.int32),
        ),
        in_specs=[smem, smem, vmem, pl.BlockSpec(memory_space=pl.ANY)],
        out_specs=(vmem, smem),
        scratch_shapes=[
            pltpu.SMEM((count,), jnp.int32),
            pltpu.SMEM((pairs + 1,), jnp.int32),
            pltpu.SMEM((pairs + 1,), jnp.int32),
            pltpu.VMEM((pairs, size, size), panel.dtype),
            pltpu.SemaphoreType.DMA((pairs,)),
        ],
        name="square_products",
    )(left_cols, panel_cols, left, panel.reshape(count * slots, size, size))


def exchange_kernel(size, part, rows, landed, rows_landed, own, send, recv, row_send, row_recv):
    me = lax.axis_index("gz")
    greet(("gz",))
    copies = [
        pltpu.make_async_copy(part.at[me], landed.at[me], own.at[0]),
        pltpu.make_async_copy(rows, rows_landed.at[me], own.at[1]),
    ]
    for d in range(1, size):
        peer = lax.rem(me + d, size)
        copies.append(remote(part.at[peer], landed.at[me], send.at[d - 1], recv.at[d - 1], "gz", peer))
        copies.append(
            remote(rows, rows_landed.at[me], row_send.at[d - 1], row_recv.at[d - 1], "gz", peer)
        )
    for copy in copies:
        copy.start()
    for copy in copies:
        copy.wait()


def exchange(part, rows):
    size = lax.axis_size("gz")
    dma = pltpu.SemaphoreType.DMA
    vmem = pl.BlockSpec(memory_space=pltpu.VMEM)
    return pl.pallas_call(
        functools.partial(exchange_kernel, size),
        out_shape=(
            jax.ShapeDtypeStruct(part.shape, part.dtype),
            jax.ShapeDtypeStruct((size,) + rows.shape, rows.dtype),
        ),
        in_specs=[vmem, vmem],
        out_specs=(vmem, vmem),
        scratch_shapes=[dma((2,))] + [dma((size - 1,))] * 4,
        compiler_params=pltpu.CompilerParams(collective_id=1, has_side_effects=True),
        name="square_exchange",
    )(part, rows)


def sum_kernel(rows, landed, out, total):
    total[...] = jnp.zeros_like(total)
    for b in range(landed.shape[0]):
        for n in range(landed.shape[1]):
            total[rows[b, 0, n]] += landed[b, n].astype(jnp.float32)
    out[...] = total[...].astype(out.dtype)


def sum_products(landed, rows, count):
    shape = (count,) + landed.shape[2:]
    vmem = pl.BlockSpec(memory_space=pltpu.VMEM)
    return pl.pallas_call(
        sum_kernel,
        out_shape=jax.ShapeDtypeStruct(shape, landed.dtype),
        in_specs=[pl.BlockSpec(memory_space=pltpu.SMEM), vmem],
        out_specs=vmem,
        scratch_shapes=[pltpu.VMEM(shape, jnp.float32)],
        name="square_sum",
    )(rows, landed)


def spread_kernel(size, pieces, chunk, out, own, send, recv):
    me = lax.axis_index("gz")
    rows = chunk.shape[0] // pieces
    greet(("gz",))
    keep = pltpu.make_async_copy(chunk, out.at[me], own)
    keep.start()

    def hop(side, step, p):
        way = 1 - 2 * side
        block = me - way * step
        span = pl.ds(p * rows, rows)
        source = chunk.at[span] if step == 0 else out.at[block, span]
        copy = remote(source, out.at[block, span], send.at[side, step, p], recv.at[side, step, p],
                      "gz", lax.rem(me + way + size, size))
        ahead = me + way
        valid = (block >= 0) & (block < size) & (ahead >= 0) & (ahead < size)
        return copy, valid

    def landing(side, step, p):
        way = 1 - 2 * side
        block = me - way * (step + 1)
        span = pl.ds(p * rows, rows)
        copy = remote(out.at[block, span], out.at[block, span], send.at[side, step, p],
                      recv.at[side, step, p], "gz", lax.rem(me + way + size, size))
        return copy, (block >= 0) & (block < size)

    def send_hop(side, step, p):
        copy, valid = hop(side, step, p)

        @pl.when(valid)
        def _():
            copy.start()

    for p in range(pieces):
        for side in range(2):
            send_hop(side, 0, p)
    for step in range(size - 1):
        for p in range(pieces):
            for side in range(2):
                copy, valid = landing(side, step, p)

                @pl.when(valid)
                def _():
                    copy.wait_recv()

                if step + 1 < size - 1:
                    send_hop(side, step + 1, p)
    for step in range(size - 1):
        for p in range(pieces):
            for side in range(2):
                copy, valid = hop(side, step, p)

                @pl.when(valid)
                def _():
                    copy.wait_send()
    keep.wait()


def spread(chunk):
    size = lax.axis_size("gz")
    pieces = pieces_of(chunk.shape[0], 8)
    dma = pltpu.SemaphoreType.DMA
    vmem = pl.BlockSpec(memory_space=pltpu.VMEM)
    return pl.pallas_call(
        functools.partial(spread_kernel, size, pieces),
        out_shape=jax.ShapeDtypeStruct((size,) + chunk.shape, chunk.dtype),
        in_specs=[vmem],
        out_specs=vmem,
        scratch_shapes=[dma, dma((2, size - 1, pieces)), dma((2, size - 1, pieces))],
        compiler_params=pltpu.CompilerParams(collective_id=3, has_side_effects=True),
        name="square_spread",
    )(chunk)


def second_kernel(block, slots, groups, panel_cols, square, tiles, out, total):
    step = pl.program_id(0)
    count = total.shape[0]
    height = total.shape[1] // groups

    def rows_of(c):
        return jnp.concatenate([square[q, c] for q in range(square.shape[0])], axis=0)

    @pl.when(step == 0)
    def _():
        total[...] = jnp.zeros_like(total)

    for r in range(block):
        row = step * block + r
        base = row * slots
        rounded = rows_of(row)
        for k in range(0, slots, 2):
            held = jnp.concatenate([tiles[r, j] for j in range(k, min(k + 2, slots))], axis=1)
            product = jnp.dot(rounded, held, preferred_element_type=jnp.float32)
            for j in range(k, min(k + 2, slots)):
                width = tiles.shape[3]
                total[panel_cols[base + j]] += product[:, (j - k) * width:(j - k + 1) * width]

    @pl.when(step == pl.num_programs(0) - 1)
    def _():
        same = (lax.axis_index("gy") == lax.axis_index("gz")).astype(jnp.float32)

        @pl.loop(0, count)
        def _(c):
            value = (3.0 * same) * rows_of(c).astype(jnp.float32) - 2.0 * total[c]
            value = value.astype(out.dtype)
            for g in range(groups):
                out[g, c] = value[g * height:(g + 1) * height]


def second(square, panel, panel_cols):
    count, slots, size = panel.shape[0], panel.shape[1], panel.shape[2]
    groups = lax.axis_size("gy")
    block = pieces_of(count, 8)
    shape = (groups, count, size // groups, size)
    return pl.pallas_call(
        functools.partial(second_kernel, block, slots, groups),
        out_shape=jax.ShapeDtypeStruct(shape, panel.dtype),
        grid=(count // block,),
        in_specs=[
            pl.BlockSpec(memory_space=pltpu.SMEM),
            pl.BlockSpec(square.shape, lambda i: (0, 0, 0, 0)),
            pl.BlockSpec((block, slots, size, size), lambda i: (i, 0, 0, 0)),
        ],
        out_specs=pl.BlockSpec(shape, lambda i: (0, 0, 0, 0)),
        scratch_shapes=[pltpu.VMEM((count, size, size), jnp.float32)],
        compiler_params=pltpu.CompilerParams(dimension_semantics=("arbitrary",)),
        name="cube_partial",
    )(panel_cols, square, panel)


def scatter_kernel(size, pieces, part, out, landed, send, recv):
    me = lax.axis_index("gy")
    rows = part.shape[1] // pieces
    width = part.shape[3]
    greet(("gy",))
    copies = []
    for p in range(pieces):
        span = pl.ds(p * rows, rows)
        for d in range(1, size):
            peer = lax.rem(me + d, size)
            copy = remote(part.at[peer, span], landed.at[d - 1, p],
                          send.at[d - 1, p], recv.at[d - 1, p], "gy", peer)
            copy.start()
            copies.append(copy)
    for p in range(pieces):
        for d in range(1, size):
            copies[p * (size - 1) + d - 1].wait_recv()
        for r in range(rows):
            c = p * rows + r
            total = part[me, c].astype(jnp.float32)
            for d in range(1, size):
                total = total + landed[d - 1, p, r].astype(jnp.float32)
            out[:, c * width:(c + 1) * width] = total
    for copy in copies:
        copy.wait_send()


def scatter_result(part):
    size = lax.axis_size("gy")
    count, height, width = part.shape[1:]
    pieces = pieces_of(count, 8)
    dma = pltpu.SemaphoreType.DMA
    return pl.pallas_call(
        functools.partial(scatter_kernel, size, pieces),
        out_shape=jax.ShapeDtypeStruct((height, count * width), jnp.float32),
        in_specs=[pl.BlockSpec(memory_space=pltpu.VMEM)],
        out_specs=pl.BlockSpec(memory_space=pltpu.VMEM),
        scratch_shapes=[
            pltpu.VMEM((size - 1, pieces, count // pieces, height, width), part.dtype),
            dma((size - 1, pieces)), dma((size - 1, pieces)),
        ],
        compiler_params=pltpu.CompilerParams(collective_id=2, has_side_effects=True),
        name="result_scatter",
    )(part)


def local(block_values, block_cols):
    tiles = block_values[0, :, 0]
    cols = block_cols[0, :, 0]
    slots = cols.shape[1]
    panel, panel_cols, left, left_cols = gather(tiles, cols)
    panel_cols = panel_cols[:, :, :slots].reshape(-1)
    part, rows = first(left[0], left_cols, panel, panel_cols)
    landed, rows = exchange(part, rows)
    square = spread(sum_products(landed, rows, panel.shape[0]))
    return scatter_result(second(square, panel, panel_cols))


def solution(mesh):
    in_specs = (P("gy", "gx", "gz", None, None, None), P("gy", "gx", "gz", None))
    out_specs = P(("gx", "gy"), "gz")
    return jax.shard_map(local, mesh=mesh, in_specs=in_specs, out_specs=out_specs, check_vma=False)
```

profile of v0, /device:TPU:0, one launch (start us, length us, event | category | flops | bytes accessed | tf_op | source)
XLA Modules:
  0.0 141.5 jit_solution(13044209011951206779)
XLA Ops:
  0.0 0.8 copy.4
  0.8 0.6 pad.4.cols
  1.4 15.0 %gather_tiles.1 = (bf16[64,6,128,128]{3,2,1,0:T(8,128)(2,1)}, s32[2,32,128]{2,1,0:T(8,128)}, bf16[1,6,128,128]{3,2,1,0:T(8,128)(2,1)}, s32[32,128]{1,0:T(8,128)}) custom-call(bf16[32,6,128,128]{3,2,1,0:T(8,128)(2,1)} %bitcast.6, s32[32,128]{1,0:T(8,128)} %pad.4.cols), custom_call_target="tpu_custom_call" | custom-call | tf_op jit(solution)/shard_map/gather_tiles/pallas_call | solution.py:109
  16.3 1.5 %reshape.6.panel_cols = s32[384]{0:T(512)} reshape(s32[2,32,6]{2,1,0:T(8,128)} %bitcast.9) | data formatting | bytes 3072 | tf_op jit(solution)/shard_map/reshape | solution.py:442
  17.8 6.4 %square_products.1 = (bf16[4,36,32,128]{3,2,1,0:T(8,128)(2,1)}, s32[1,128]{1,0:T(1,128)}) custom-call(s32[32,128]{1,0:T(8,128)} %get-tuple-element.14.left_cols, s32[384]{0:T(512)} %reshape.6.panel_cols, bf16[6,128,128]{2,1,0:T(8,128)(2,1)} %bitcast.7, bf16[384,128,128]{2,1,0:T(8,128)(2,1)} %bitcast.5), custom_call_target="tpu_custom_call" | custom-call | tf_op jit(solution)/shard_map/square_products/pallas_call | solution.py:184
  24.2 26.6 %square_exchange.1 = (bf16[4,36,32,128]{3,2,1,0:T(8,128)(2,1)}, s32[4,1,128]{2,1,0:T(1,128)}) custom-call(bf16[4,36,32,128]{3,2,1,0:T(8,128)(2,1)} %get-tuple-element.17.part, s32[1,128]{1,0:T(1,128)} %get-tuple-element.18.rows), custom_call_target="tpu_custom_call" | custom-call | tf_op jit(solution)/shard_map/square_exchange/pallas_call | solution.py:226
  50.8 2.9 %square_sum.1.chunk = bf16[64,32,128]{2,1,0:T(8,128)(2,1)} custom-call(s32[4,1,128]{2,1,0:T(1,128)} %get-tuple-element.19.rows, bf16[4,36,32,128]{3,2,1,0:T(8,128)(2,1)} %get-tuple-element.20.landed), custom_call_target="tpu_custom_call" | custom-call | tf_op jit(solution)/shard_map/square_sum/pallas_call | solution.py:251
  53.7 46.3 %square_spread.1.square = bf16[4,64,32,128]{3,2,1,0:T(8,128)(2,1)} custom-call(bf16[64,32,128]{2,1,0:T(8,128)(2,1)} %square_sum.1.chunk), custom_call_target="tpu_custom_call" | custom-call | tf_op jit(solution)/shard_map/square_spread/pallas_call | solution.py:324
  100.0 12.3 %cube_partial.1.part = bf16[4,64,32,128]{3,2,1,0:T(8,128)(2,1)} custom-call(s32[384]{0:T(512)} %reshape.6.panel_cols, bf16[4,64,32,128]{3,2,1,0:T(8,128)(2,1)} %square_spread.1.square, bf16[64,6,128,128]{3,2,1,0:T(8,128)(2,1)} %get-tuple-element.16.tiles), custom_call_target="tpu_custom_call" | custom-call | tf_op jit(solution)/shard_map/cube_partial/pallas_call | solution.py:375
  112.4 26.9 %result_scatter.1 = f32[32,8192]{1,0:T(8,128)} custom-call(bf16[4,64,32,128]{3,2,1,0:T(8,128)(2,1)} %cube_partial.1.part), custom_call_target="tpu_custom_call" | custom-call | tf_op jit(solution)/shard_map/result_scatter/pallas_call | solution.py:423
  139.3 2.3 %copy.6 = f32[32,8192]{1,0:T(8,128)} copy(f32[32,8192]{1,0:T(8,128)} %result_scatter.1) | data formatting | bytes 2097152
where the time goes:
time: 142 us
  Pallas kernels  136 us (96%)
  local copies, waits for them, and re-layouts  5.1 us (4%)
    pallas_call x1, Pallas kernels, spread(): pl.pallas_call(functools.partial(spread_kernel, size, pieces), out_shape=...  46.3 us
    pallas_call x1, Pallas kernels, scatter_result(): pl.pallas_call(functools.partial(scatter_kernel, size, pieces), out_shape...  26.9 us
    pallas_call x1, Pallas kernels, exchange(): pl.pallas_call(functools.partial(exchange_kernel, size), out_shape=(jax.S...  26.6 us
    pallas_call x1, Pallas kernels, gather(): pl.pallas_call(functools.partial(gather_kernel, n_gx, n_gy, pieces), out_...  15 us
    pallas_call x1, Pallas kernels, second(): pl.pallas_call(functools.partial(second_kernel, block, slots, groups), ou...  12.3 us
    pallas_call x1, Pallas kernels, first(): pl.pallas_call(functools.partial(first_kernel, slots, pairs), out_shape=(...  6.35 us
    unnamed x2, local copies, waits for them, and re-layouts  3.03 us
    pallas_call x1, Pallas kernels, sum_products(): pl.pallas_call(sum_kernel, out_shape=jax.ShapeDtypeStruct(shape, landed.d...  2.91 us

commit v1 on v0

v1 whole, which is shorter than its diff:
```python
import functools

import jax
import jax.numpy as jnp
from jax import lax
from jax.experimental import pallas as pl
from jax.experimental.pallas import tpu as pltpu
from jax.sharding import PartitionSpec as P

LANES = 128
SUB = 8
MESH = pl.DeviceIdType.MESH
HOP_LAG, SIDE_LAG, LAST_LAG = 3, 2, 3
PIECES = 8


def pieces_of(count, most):
    for pieces in range(min(count, most), 0, -1):
        if count % pieces == 0:
            return pieces


def greet(axes):
    barrier = pltpu.get_barrier_semaphore()
    total = 0
    for axis in axes:
        size = lax.axis_size(axis)
        me = lax.axis_index(axis)
        for step in range(1, size):
            pl.semaphore_signal(
                barrier, inc=1, device_id={axis: lax.rem(me + step, size)}, device_id_type=MESH
            )
        total += size - 1
    pl.semaphore_wait(barrier, total)


def remote(src, dst, send, recv, axis, peer):
    return pltpu.make_async_remote_copy(
        src_ref=src, dst_ref=dst, send_sem=send, recv_sem=recv,
        device_id={axis: peer}, device_id_type=MESH,
    )


def step_kernel(
    n_gx, n_gy, n_gz, slots, pieces, buffers,
    tiles, cols, out,
    held, window, current, heads, table_v, lists_v, table, lists,
    own, right_out, left_out, right_in, left_in, square, rounded,
    product, side_out, side_in, mixed, last_out, last_in,
    load_sem, head_sem, head_side, win_send, win_recv, fan_send, fan_recv, table_sem,
    right_send, left_send, right_recv, left_recv, side_send, side_recv, last_send, last_recv, credit,
):
    gx, gy, gz = lax.axis_index("gx"), lax.axis_index("gy"), lax.axis_index("gz")
    rows = tiles.shape[0]
    size = tiles.shape[2]
    count = n_gx * rows
    chunks = window.shape[0]
    high = n_gy * SUB
    wide = rows // pieces
    broad = count // pieces
    steps = chunks * pieces
    f32, bf16 = jnp.float32, jnp.bfloat16

    first_load = pltpu.make_async_copy(tiles.at[0], held.at[pl.ds(0, slots)], load_sem.at[0])
    first_load.start()
    loads = [first_load]
    for r in range(1, rows):
        loads.append(pltpu.make_async_copy(tiles.at[r], held.at[pl.ds(r * slots, slots)], load_sem.at[r]))
        loads[-1].start()
    greet(("gx", "gy", "gz"))

    def win_copy(m, peer):
        return remote(window.at[m, gx], window.at[m, gx], win_send.at[m, peer], win_recv.at[m], "gy", peer)

    def fan_copy(m, d):
        return remote(window.at[m, gx], window.at[m, gx], fan_send.at[m, d - 1], fan_recv.at[m, d - 1],
                      "gx", lax.rem(gx + d, n_gx))

    def fan_landing(m, d):
        g = lax.rem(gx - d + n_gx, n_gx)
        return remote(window.at[m, g], window.at[m, g], fan_send.at[m, d - 1], fan_recv.at[m, d - 1],
                      "gx", lax.rem(gx + d, n_gx))

    def head_copy(peer):
        return remote(heads.at[gx], heads.at[gx], head_sem.at[0, peer], head_sem.at[1, 0], "gy", peer)

    def head_fan(d):
        return remote(heads.at[gx], heads.at[gx], head_side.at[0, d - 1], head_side.at[1, d - 1],
                      "gx", lax.rem(gx + d, n_gx))

    def head_landing(d):
        g = lax.rem(gx - d + n_gx, n_gx)
        return remote(heads.at[g], heads.at[g], head_side.at[0, d - 1], head_side.at[1, d - 1],
                      "gx", lax.rem(gx + d, n_gx))

    @pl.when(gy == 0)
    def _():
        heads[gx] = cols[pl.ds(0, heads.shape[1])]
        for peer in range(1, n_gy):
            head_copy(peer).start()
        for d in range(1, n_gx):
            head_fan(d).start()
        first_load.wait()
        for k in range(slots):
            tile = held[k].astype(f32)
            for m in range(chunks):
                window[m, gx, k] = jnp.concatenate(
                    [tile[q * chunks * SUB + m * SUB:][:SUB] for q in range(n_gy)], axis=0
                ).astype(bf16)
        for m in range(chunks):
            for peer in range(1, n_gy):
                win_copy(m, peer).start()
            for d in range(1, n_gx):
                fan_copy(m, d).start()

    lanes = lax.broadcasted_iota(jnp.int32, (rows, LANES), 1)
    places = lax.broadcasted_iota(jnp.int32, (rows, LANES), 0)
    listed = cols[...]
    marks = [
        jnp.where(jnp.broadcast_to(listed[:, k:k + 1], (rows, LANES)) == lanes, places * SUB + k, -1)
        for k in range(slots)
    ]
    lists_v[...] = jnp.zeros_like(lists_v)
    for i in range(slots):
        top = marks[0]
        for k in range(1, slots):
            top = jnp.maximum(top, marks[k])
        top = jnp.max(top, axis=0, keepdims=True)
        marks = [jnp.where(mark == top, -1, mark) for mark in marks]
        row, slot = top // SUB, top % SUB
        lists_v[i:i + 1] = jnp.where(top < 0, rows, row)
        lists_v[SUB + i:SUB + i + 1] = jnp.where(top < 0, 0, row * slots + slot)
    list_copy = pltpu.make_async_copy(lists_v, lists, table_sem.at[0])
    list_copy.start()
    for g in range(n_gx):
        current[g, slots] = jnp.zeros((high, size), bf16)
    for parity in range(2):
        rounded[parity, rows] = jnp.zeros((n_gx * high, size), bf16)

    @pl.when(gy != 0)
    def _():
        head_copy(0).wait_recv()
        for d in range(1, n_gx):
            head_fan(d).start()

    for d in range(1, n_gx):
        head_landing(d).wait_recv()
    total = jnp.zeros((rows, LANES), jnp.int32)
    for g in range(n_gx):
        found = jnp.full((rows, LANES), slots, jnp.int32)
        for k in range(slots):
            found = jnp.where(listed == jnp.broadcast_to(heads[g, 0:1, k:k + 1], (rows, LANES)), k, found)
        found = jnp.where(lanes < slots, found, 0)
        total = total + (found if g == 0 else pltpu.roll(found, g * SUB, 1))
    table_v[...] = total
    table_copy = pltpu.make_async_copy(table_v, table, table_sem.at[1])
    table_copy.start()

    def forward(m):
        @pl.when(gy != 0)
        def _():
            win_copy(m, 0).wait_recv()
            for d in range(1, n_gx):
                fan_copy(m, d).start()

    forward(0)
    for load in loads[1:]:
        load.wait()

    @pl.when(gy != 0)
    def _():
        first_load.wait()

    list_copy.wait()
    table_copy.wait()

    def right_copy(t):
        return remote(right_out.at[t], right_in.at[t], right_send.at[t], right_recv.at[t],
                      "gz", lax.rem(gz + 1, n_gz))

    def left_copy(t):
        return remote(left_out.at[t], left_in.at[t], left_send.at[t], left_recv.at[t],
                      "gz", lax.rem(gz + n_gz - 1, n_gz))

    def side_slot(u):
        return u if buffers == chunks else lax.rem(u, buffers * pieces)

    def side_copy(u, d):
        peer = lax.rem(gx + d, n_gx)
        s = side_slot(u)
        return remote(side_out.at[s, peer], side_in.at[s, d - 1], side_send.at[s, d - 1], side_recv.at[s, d - 1],
                      "gx", peer)

    def last_copy(v, d):
        peer = lax.rem(gy + d, n_gy)
        return remote(last_out.at[v, peer], last_in.at[v, d - 1], last_send.at[v, d - 1], last_recv.at[v, d - 1],
                      "gy", peer)

    def during(t):
        return (t >= 0) & (t < steps)

    def stage_own(t):
        m, q = t // pieces, lax.rem(t, pieces)

        @pl.when((q == 1 % pieces) & (m + 1 < chunks))
        def _():
            forward(m + 1)

        @pl.when(q == 0)
        def _():
            for d in range(1, n_gx):
                fan_landing(m, d).wait_recv()
            for g in range(n_gx):
                for k in range(slots):
                    current[g, k] = window[m, g, k]

        for i in range(wide):
            c = q * wide + i
            lhs = jnp.concatenate([
                jnp.concatenate([current[g, table[c, g * SUB + j]] for g in range(n_gx)], axis=0)
                for j in range(slots)
            ], axis=1)
            rhs = jnp.concatenate([held[c * slots + j] for j in range(slots)], axis=1)
            own[t, i] = lax.dot_general(lhs, rhs, (((1,), (1,)), ((), ())), preferred_element_type=f32)

    def stage_right(t):
        @pl.when(gz == 0)
        def _():
            right_out[t] = own[t].astype(bf16)

        @pl.when(gz > 0)
        def _():
            right_copy(t).wait_recv()

        @pl.when((gz > 0) & (gz < n_gz - 1))
        def _():
            right_out[t] = (own[t] + right_in[t].astype(f32)).astype(bf16)

        @pl.when(gz < n_gz - 1)
        def _():
            right_copy(t).start()

    def stage_left(t):
        @pl.when(gz == n_gz - 1)
        def _():
            left_out[t] = own[t].astype(bf16)

        @pl.when(gz < n_gz - 1)
        def _():
            left_copy(t).wait_recv()

        @pl.when((gz > 0) & (gz < n_gz - 1))
        def _():
            left_out[t] = (own[t] + left_in[t].astype(f32)).astype(bf16)

        @pl.when(gz > 0)
        def _():
            left_copy(t).start()

    def stage_sum(t):
        parity, q = lax.rem(t // pieces, 2), lax.rem(t, pieces)

        def keep(total):
            square[parity, pl.ds(q * wide, wide)] = total
            rounded[parity, pl.ds(q * wide, wide)] = total.astype(bf16)

        @pl.when(gz == 0)
        def _():
            keep(own[t] + left_in[t].astype(f32))

        @pl.when(gz == n_gz - 1)
        def _():
            keep(own[t] + right_in[t].astype(f32))

        @pl.when((gz > 0) & (gz < n_gz - 1))
        def _():
            keep(own[t] + right_in[t].astype(f32) + left_in[t].astype(f32))

    def stage_second(u):
        parity, q = lax.rem(u // pieces, 2), lax.rem(u, pieces)
        depth = min(slots, rows)
        s = side_slot(u)
        hold = lax.rem(u, SIDE_LAG + 1)
        if buffers < chunks:
            @pl.when((q == 0) & (u >= buffers * pieces))
            def _():
                pl.semaphore_wait(credit, n_gx - 1)

            @pl.when(u >= buffers * pieces)
            def _():
                for d in range(1, n_gx):
                    side_copy(u, d).wait_send()

        for i in range(broad):
            c = q * broad + i
            lhs = jnp.concatenate([rounded[parity, lists[j, c]] for j in range(depth)], axis=1)
            rhs = jnp.concatenate([held[lists[SUB + j, c]] for j in range(depth)], axis=0)
            near = c - gx * rows
            here = (gy == gz) & (near >= 0) & (near < rows)
            near = jnp.clip(near, 0, rows - 1)
            value = (jnp.where(here, 3.0, 0.0) * square[parity, near]
                     - 2.0 * jnp.dot(lhs, rhs, preferred_element_type=f32))
            mine = value[:high]
            for g in range(1, n_gx):
                mine = jnp.where(gx == g, value[g * high:(g + 1) * high], mine)
            product[hold, i] = mine
            for g in range(n_gx):
                side_out[s, g, i] = value[g * high:(g + 1) * high].astype(bf16)
        for d in range(1, n_gx):
            side_copy(u, d).start()

    def stage_mix(v):
        m, q = v // pieces, lax.rem(v, pieces)
        hold = lax.rem(v, SIDE_LAG + 1)
        s = side_slot(v)
        for d in range(1, n_gx):
            side_copy(v, d).wait_recv()
        for i in range(0, broad, 2):
            pair = []
            for h in range(i, i + 2):
                value = product[hold, h]
                for d in range(1, n_gx):
                    value = value + side_in[s, d - 1, h].astype(f32)
                mixed[h] = value
                pair.append(value)
            for y in range(n_gy):
                last_out[v, y, i // 2] = jnp.concatenate(
                    [value[y * SUB:(y + 1) * SUB] for value in pair], axis=0
                ).astype(bf16)
        for d in range(1, n_gy):
            last_copy(v, d).start()
        if buffers < chunks:
            @pl.when((q == pieces - 1) & (m + buffers < chunks))
            def _():
                for d in range(1, n_gx):
                    pl.semaphore_signal(credit, inc=1, device_id={"gx": lax.rem(gx + d, n_gx)},
                                        device_id_type=MESH)
        down = pl.ds(pl.multiple_of(m * SUB, SUB), SUB)
        for i in range(broad):
            across = pl.ds(pl.multiple_of((q * broad + i) * size, size), size)
            out[down, across] = mixed[i, pl.ds(pl.multiple_of(gy * SUB, SUB), SUB)]

    def stage_last(w):
        m, q = w // pieces, lax.rem(w, pieces)
        for d in range(1, n_gy):
            last_copy(w, d).wait_recv()
        down = pl.ds(pl.multiple_of(m * SUB, SUB), SUB)
        for i in range(0, broad, 2):
            value = last_in[w, 0, i // 2].astype(f32)
            for d in range(2, n_gy):
                value = value + last_in[w, d - 1, i // 2].astype(f32)
            for h in range(2):
                across = pl.ds(pl.multiple_of((q * broad + i + h) * size, size), size)
                out[down, across] += value[h * SUB:(h + 1) * SUB]

    sum_at = (n_gz - 1) * HOP_LAG
    second_at = sum_at + pieces
    mix_at = second_at + SIDE_LAG
    last_at = mix_at + LAST_LAG

    def slot(s, carry):
        for stage, delay in (
            (stage_own, 0),
            (stage_right, gz * HOP_LAG),
            (stage_left, (n_gz - 1 - gz) * HOP_LAG),
            (stage_sum, sum_at),
            (stage_mix, mix_at),
            (stage_second, second_at),
            (stage_last, last_at),
        ):
            pl.when(during(s - delay))(functools.partial(stage, s - delay))
        return carry

    lax.fori_loop(0, steps + last_at, slot, jnp.int32(0))

    @pl.loop(0, steps)
    def _(t):
        @pl.when(gz < n_gz - 1)
        def _():
            right_copy(t).wait_send()

        @pl.when(gz > 0)
        def _():
            left_copy(t).wait_send()

        for d in range(1, n_gy):
            last_copy(t, d).wait_send()

    @pl.loop(0, buffers * pieces)
    def _(t):
        for d in range(1, n_gx):
            side_copy(t, d).wait_send()

    for d in range(1, n_gx):
        head_fan(d).wait_send()
        for m in range(chunks):
            fan_copy(m, d).wait_send()

    @pl.when(gy == 0)
    def _():
        for peer in range(1, n_gy):
            head_copy(peer).wait_send()
            for m in range(chunks):
                win_copy(m, peer).wait_send()


def local(block_values, block_cols):
    n_gx, n_gy, n_gz = (lax.axis_size(a) for a in ("gx", "gy", "gz"))
    tiles = block_values[0, :, 0]
    cols = block_cols[0, :, 0]
    rows, slots, size = tiles.shape[:3]
    cols = jnp.pad(cols, ((0, 0), (0, LANES - slots)), constant_values=-1)
    count = n_gx * rows
    chunks = size // (n_gy * SUB)
    high = n_gy * SUB
    pieces = pieces_of(rows, PIECES)
    wide, broad, steps = rows // pieces, count // pieces, chunks * pieces
    tall = n_gx * high
    buffers = chunks if n_gx <= 4 else 2
    top = min(SUB, rows)
    dma = pltpu.SemaphoreType.DMA
    f32, bf16 = jnp.float32, jnp.bfloat16
    flow = (steps, wide, tall, size)
    return pl.pallas_call(
        functools.partial(step_kernel, n_gx, n_gy, n_gz, slots, pieces, buffers),
        out_shape=jax.ShapeDtypeStruct((size // n_gy, count * size), f32),
        in_specs=[pl.BlockSpec(memory_space=pl.ANY), pl.BlockSpec(memory_space=pltpu.VMEM)],
        out_specs=pl.BlockSpec(memory_space=pltpu.VMEM),
        scratch_shapes=[
            pltpu.VMEM((rows * slots, size, size), bf16),
            pltpu.VMEM((chunks, n_gx, slots, high, size), bf16),
            pltpu.VMEM((n_gx, slots + 1, high, size), bf16),
            pltpu.VMEM((n_gx, top, LANES), jnp.int32),
            pltpu.VMEM((rows, LANES), jnp.int32),
            pltpu.VMEM((2 * SUB, LANES), jnp.int32),
            pltpu.SMEM((rows, LANES), jnp.int32),
            pltpu.SMEM((2 * SUB, LANES), jnp.int32),
            pltpu.VMEM(flow, f32),
            pltpu.VMEM(flow, bf16), pltpu.VMEM(flow, bf16), pltpu.VMEM(flow, bf16), pltpu.VMEM(flow, bf16),
            pltpu.VMEM((2, rows, tall, size), f32),
            pltpu.VMEM((2, rows + 1, tall, size), bf16),
            pltpu.VMEM((SIDE_LAG + 1, broad, high, size), f32),
            pltpu.VMEM((buffers * pieces, n_gx, broad, high, size), bf16),
            pltpu.VMEM((buffers * pieces, n_gx - 1, broad, high, size), bf16),
            pltpu.VMEM((broad, high, size), f32),
            pltpu.VMEM((steps, n_gy, broad // 2, 2 * SUB, size), bf16),
            pltpu.VMEM((steps, n_gy - 1, broad // 2, 2 * SUB, size), bf16),
            dma((rows,)), dma((2, n_gy)), dma((2, n_gx - 1)),
            dma((chunks, n_gy)), dma((chunks,)), dma((chunks, n_gx - 1)), dma((chunks, n_gx - 1)), dma((2,)),
            dma((steps,)), dma((steps,)), dma((steps,)), dma((steps,)),
            dma((buffers * pieces, n_gx - 1)), dma((buffers * pieces, n_gx - 1)),
            dma((steps, n_gy - 1)), dma((steps, n_gy - 1)),
            pltpu.SemaphoreType.REGULAR,
        ],
        compiler_params=pltpu.CompilerParams(
            collective_id=0, has_side_effects=True, vmem_limit_bytes=67043328
        ),
        name="purify",
    )(tiles, cols)


def solution(mesh):
    in_specs = (P("gy", "gx", "gz", None, None, None), P("gy", "gx", "gz", None))
    out_specs = P(("gx", "gy"), "gz")
    return jax.shard_map(local, mesh=mesh, in_specs=in_specs, out_specs=out_specs, check_vma=False)
```

time: 142 us -> 88.3 us (0.62)
  Pallas kernels: 136 us -> 84.4 us
  local copies, waits for them, and re-layouts: 5.1 us -> 3.64 us
    pallas_call x7 -> x1, Pallas kernels: 136 us -> 84.4 us  [local(): pl.pallas_call(functools.partial(step_kernel, n_gx, n_gy, n_gz, slots, pi...]
    reshape x1 -> x0, local copies, waits for them, and re-layouts: 1.46 us -> none  [local(): panel_cols = panel_cols[:, :, :slots].reshape(-1)]
where the time goes in v1:
time: 88.3 us; the launch traced here: 88 us
  Pallas kernels  84.4 us (96%)
  local copies, waits for them, and re-layouts  3.64 us (4%)
    pallas_call x1, Pallas kernels, local(): pl.pallas_call(functools.partial(step_kernel, n_gx, n_gy, n_gz, slots, pi...  84.4 us
    unnamed x2, local copies, waits for them, and re-layouts  3.03 us

profile of v1, /device:TPU:0, one launch (start us, length us, event | category | flops | bytes accessed | tf_op | source)
XLA Modules:
  0.0 88.0 jit_solution(3081633892970496866)
XLA Ops:
  0.0 0.8 copy.3
  0.8 0.6 pad.4.cols
  1.4 84.4 %purify.1 = f32[32,8192]{1,0:T(8,128)} custom-call(bf16[32,6,128,128]{3,2,1,0:T(8,128)(2,1)} %bitcast.2, s32[32,128]{1,0:T(8,128)} %pad.4.cols), custom_call_target="tpu_custom_call" | custom-call | tf_op jit(solution)/shard_map/purify/pallas_call | solution.py:424
  85.8 2.3 %copy.5 = f32[32,8192]{1,0:T(8,128)} copy(f32[32,8192]{1,0:T(8,128)} %purify.1) | data formatting | bytes 2097152

commit v2 on v1

--- a/solution.py
+++ b/solution.py
@@ -9,8 +9,9 @@
 
 LANES = 128
 SUB = 8
+VMEM = 67043328
 MESH = pl.DeviceIdType.MESH
-HOP_LAG, SIDE_LAG, LAST_LAG = 3, 2, 3
+HOP_LAG, SIDE_LAG, LAST_LAG = 3, 2, 6
 PIECES = 8
 
 
@@ -51,7 +52,7 @@
     right_send, left_send, right_recv, left_recv, side_send, side_recv, last_send, last_recv, credit,
 ):
     gx, gy, gz = lax.axis_index("gx"), lax.axis_index("gy"), lax.axis_index("gz")
-    rows = tiles.shape[0]
+    rows = cols.shape[3]
     size = tiles.shape[2]
     count = n_gx * rows
     chunks = window.shape[0]
@@ -61,24 +62,29 @@
     steps = chunks * pieces
     f32, bf16 = jnp.float32, jnp.bfloat16
 
-    first_load = pltpu.make_async_copy(tiles.at[0], held.at[pl.ds(0, slots)], load_sem.at[0])
+    first_load = pltpu.make_async_copy(tiles.at[pl.ds(0, slots)], held.at[pl.ds(0, slots)], load_sem.at[0])
     first_load.start()
     loads = [first_load]
-    for r in range(1, rows):
-        loads.append(pltpu.make_async_copy(tiles.at[r], held.at[pl.ds(r * slots, slots)], load_sem.at[r]))
+    parts = load_sem.shape[0] - 1
+    for part in range(parts):
+        low, top = 1 + (rows - 1) * part // parts, 1 + (rows - 1) * (part + 1) // parts
+        loads.append(pltpu.make_async_copy(
+            tiles.at[pl.ds(low * slots, (top - low) * slots)], held.at[pl.ds(low * slots, (top - low) * slots)],
+            load_sem.at[part + 1],
+        ))
         loads[-1].start()
     greet(("gx", "gy", "gz"))
 
     def win_copy(m, peer):
-        return remote(window.at[m, gx], window.at[m, gx], win_send.at[m, peer], win_recv.at[m], "gy", peer)
+        return remote(window.at[m, gx], window.at[m, gx], win_send.at[peer], win_recv.at[m], "gy", peer)
 
     def fan_copy(m, d):
-        return remote(window.at[m, gx], window.at[m, gx], fan_send.at[m, d - 1], fan_recv.at[m, d - 1],
+        return remote(window.at[m, gx], window.at[m, gx], fan_send.at[d - 1], fan_recv.at[m, d - 1],
                       "gx", lax.rem(gx + d, n_gx))
 
     def fan_landing(m, d):
         g = lax.rem(gx - d + n_gx, n_gx)
-        return remote(window.at[m, g], window.at[m, g], fan_send.at[m, d - 1], fan_recv.at[m, d - 1],
+        return remote(window.at[m, g], window.at[m, g], fan_send.at[d - 1], fan_recv.at[m, d - 1],
                       "gx", lax.rem(gx + d, n_gx))
 
     def head_copy(peer):
@@ -93,9 +99,17 @@
         return remote(heads.at[g], heads.at[g], head_side.at[0, d - 1], head_side.at[1, d - 1],
                       "gx", lax.rem(gx + d, n_gx))
 
+    lanes = lax.broadcasted_iota(jnp.int32, (rows, LANES), 1)
+    places = lax.broadcasted_iota(jnp.int32, (rows, LANES), 0)
+    listed = cols[0, :, 0, :].T
+    each = [jnp.broadcast_to(listed[:, k:k + 1], (rows, LANES)) for k in range(slots)]
+    spread = jnp.full((rows, LANES), -1, jnp.int32)
+    for k in range(slots):
+        spread = jnp.where(lanes == k, each[k], spread)
+
     @pl.when(gy == 0)
     def _():
-        heads[gx] = cols[pl.ds(0, heads.shape[1])]
+        heads[gx] = spread[:heads.shape[1]]
         for peer in range(1, n_gy):
             head_copy(peer).start()
         for d in range(1, n_gx):
@@ -113,13 +127,7 @@
             for d in range(1, n_gx):
                 fan_copy(m, d).start()
 
-    lanes = lax.broadcasted_iota(jnp.int32, (rows, LANES), 1)
-    places = lax.broadcasted_iota(jnp.int32, (rows, LANES), 0)
-    listed = cols[...]
-    marks = [
-        jnp.where(jnp.broadcast_to(listed[:, k:k + 1], (rows, LANES)) == lanes, places * SUB + k, -1)
-        for k in range(slots)
-    ]
+    marks = [jnp.where(each[k] == lanes, places * SUB + k, -1) for k in range(slots)]
     lists_v[...] = jnp.zeros_like(lists_v)
     for i in range(slots):
         top = marks[0]
@@ -149,7 +157,7 @@
     for g in range(n_gx):
         found = jnp.full((rows, LANES), slots, jnp.int32)
         for k in range(slots):
-            found = jnp.where(listed == jnp.broadcast_to(heads[g, 0:1, k:k + 1], (rows, LANES)), k, found)
+            found = jnp.where(spread == jnp.broadcast_to(heads[g, 0:1, k:k + 1], (rows, LANES)), k, found)
         found = jnp.where(lanes < slots, found, 0)
         total = total + (found if g == 0 else pltpu.roll(found, g * SUB, 1))
     table_v[...] = total
@@ -175,25 +183,36 @@
     table_copy.wait()
 
     def right_copy(t):
-        return remote(right_out.at[t], right_in.at[t], right_send.at[t], right_recv.at[t],
+        return remote(right_out.at[t], right_in.at[t], right_send, right_recv.at[t],
                       "gz", lax.rem(gz + 1, n_gz))
 
     def left_copy(t):
-        return remote(left_out.at[t], left_in.at[t], left_send.at[t], left_recv.at[t],
+        return remote(left_out.at[t], left_in.at[t], left_send, left_recv.at[t],
                       "gz", lax.rem(gz + n_gz - 1, n_gz))
 
     def side_slot(u):
         return u if buffers == chunks else lax.rem(u, buffers * pieces)
+
+    def side_sem(s):
+        return 0 if buffers == chunks else s
+
+    def side_all(u):
+        s = side_slot(u)
+        return remote(side_in.at[s], side_in.at[s], side_send.at[side_sem(s)], side_recv.at[s],
+                      "gx", lax.rem(gx + 1, n_gx))
+
+    def last_all(v):
+        return remote(last_in.at[v], last_in.at[v], last_send, last_recv.at[v], "gy", lax.rem(gy + 1, n_gy))
 
     def side_copy(u, d):
         peer = lax.rem(gx + d, n_gx)
         s = side_slot(u)
-        return remote(side_out.at[s, peer], side_in.at[s, d - 1], side_send.at[s, d - 1], side_recv.at[s, d - 1],
+        return remote(side_out.at[s, peer], side_in.at[s, d - 1], side_send.at[side_sem(s)], side_recv.at[s],
                       "gx", peer)
 
     def last_copy(v, d):
         peer = lax.rem(gy + d, n_gy)
-        return remote(last_out.at[v, peer], last_in.at[v, d - 1], last_send.at[v, d - 1], last_recv.at[v, d - 1],
+        return remote(last_out.at[v, peer], last_in.at[v, d - 1], last_send, last_recv.at[v],
                       "gy", peer)
 
     def during(t):
@@ -288,8 +307,7 @@
 
             @pl.when(u >= buffers * pieces)
             def _():
-                for d in range(1, n_gx):
-                    side_copy(u, d).wait_send()
+                side_all(u).wait_send()
 
         for i in range(broad):
             c = q * broad + i
@@ -313,8 +331,7 @@
         m, q = v // pieces, lax.rem(v, pieces)
         hold = lax.rem(v, SIDE_LAG + 1)
         s = side_slot(v)
-        for d in range(1, n_gx):
-            side_copy(v, d).wait_recv()
+        side_all(v).wait_recv()
         for i in range(0, broad, 2):
             pair = []
             for h in range(i, i + 2):
@@ -342,8 +359,7 @@
 
     def stage_last(w):
         m, q = w // pieces, lax.rem(w, pieces)
-        for d in range(1, n_gy):
-            last_copy(w, d).wait_recv()
+        last_all(w).wait_recv()
         down = pl.ds(pl.multiple_of(m * SUB, SUB), SUB)
         for i in range(0, broad, 2):
             value = last_in[w, 0, i // 2].astype(f32)
@@ -373,43 +389,40 @@
 
     lax.fori_loop(0, steps + last_at, slot, jnp.int32(0))
 
-    @pl.loop(0, steps)
-    def _(t):
-        @pl.when(gz < n_gz - 1)
-        def _():
-            right_copy(t).wait_send()
-
-        @pl.when(gz > 0)
-        def _():
-            left_copy(t).wait_send()
-
-        for d in range(1, n_gy):
-            last_copy(t, d).wait_send()
-
-    @pl.loop(0, buffers * pieces)
-    def _(t):
-        for d in range(1, n_gx):
-            side_copy(t, d).wait_send()
+    @pl.when(gz < n_gz - 1)
+    def _():
+        remote(right_out, right_out, right_send, right_recv.at[0], "gz", lax.rem(gz + 1, n_gz)).wait_send()
+
+    @pl.when(gz > 0)
+    def _():
+        remote(left_out, left_out, left_send, left_recv.at[0], "gz", lax.rem(gz + n_gz - 1, n_gz)).wait_send()
+
+    remote(last_in, last_in, last_send, last_recv.at[0], "gy", lax.rem(gy + 1, n_gy)).wait_send()
+    if buffers == chunks:
+        remote(side_in, side_in, side_send.at[0], side_recv.at[0], "gx", lax.rem(gx + 1, n_gx)).wait_send()
+    else:
+        @pl.loop(0, buffers * pieces)
+        def _(t):
+            side_all(t).wait_send()
 
     for d in range(1, n_gx):
         head_fan(d).wait_send()
-        for m in range(chunks):
-            fan_copy(m, d).wait_send()
+        whole = window.at[:, gx]
+        remote(whole, whole, fan_send.at[d - 1], fan_recv.at[0, d - 1], "gx", lax.rem(gx + d, n_gx)).wait_send()
 
     @pl.when(gy == 0)
     def _():
         for peer in range(1, n_gy):
             head_copy(peer).wait_send()
-            for m in range(chunks):
-                win_copy(m, peer).wait_send()
+            whole = window.at[:, gx]
+            remote(whole, whole, win_send.at[peer], win_recv.at[0], "gy", peer).wait_send()
 
 
 def local(block_values, block_cols):
     n_gx, n_gy, n_gz = (lax.axis_size(a) for a in ("gx", "gy", "gz"))
-    tiles = block_values[0, :, 0]
-    cols = block_cols[0, :, 0]
-    rows, slots, size = tiles.shape[:3]
-    cols = jnp.pad(cols, ((0, 0), (0, LANES - slots)), constant_values=-1)
+    rows, slots = block_cols.shape[1], block_cols.shape[3]
+    size = block_values.shape[4]
+    tiles = block_values.reshape(rows * slots, size, size)
     count = n_gx * rows
     chunks = size // (n_gy * SUB)
     high = n_gy * SUB
@@ -418,6 +431,7 @@
     tall = n_gx * high
     buffers = chunks if n_gx <= 4 else 2
     top = min(SUB, rows)
+    limit = VMEM if buffers < chunks else VMEM - 4 * rows * slots * size * size
     dma = pltpu.SemaphoreType.DMA
     f32, bf16 = jnp.float32, jnp.bfloat16
     flow = (steps, wide, tall, size)
@@ -445,18 +459,18 @@
             pltpu.VMEM((broad, high, size), f32),
             pltpu.VMEM((steps, n_gy, broad // 2, 2 * SUB, size), bf16),
             pltpu.VMEM((steps, n_gy - 1, broad // 2, 2 * SUB, size), bf16),
-            dma((rows,)), dma((2, n_gy)), dma((2, n_gx - 1)),
-            dma((chunks, n_gy)), dma((chunks,)), dma((chunks, n_gx - 1)), dma((chunks, n_gx - 1)), dma((2,)),
-            dma((steps,)), dma((steps,)), dma((steps,)), dma((steps,)),
-            dma((buffers * pieces, n_gx - 1)), dma((buffers * pieces, n_gx - 1)),
-            dma((steps, n_gy - 1)), dma((steps, n_gy - 1)),
+            dma((1 + min(4, rows - 1),)), dma((2, n_gy)), dma((2, n_gx - 1)),
+            dma((n_gy,)), dma((chunks,)), dma((n_gx - 1,)), dma((chunks, n_gx - 1)), dma((2,)),
+            dma, dma, dma((steps,)), dma((steps,)),
+            dma((1 if buffers == chunks else buffers * pieces,)), dma((buffers * pieces,)),
+            dma, dma((steps,)),
             pltpu.SemaphoreType.REGULAR,
         ],
         compiler_params=pltpu.CompilerParams(
-            collective_id=0, has_side_effects=True, vmem_limit_bytes=67043328
+            collective_id=0, has_side_effects=True, vmem_limit_bytes=limit
         ),
         name="purify",
-    )(tiles, cols)
+    )(tiles, jnp.transpose(block_cols, (0, 3, 2, 1)))
 
 
 def solution(mesh):

time: 88.3 us -> 79.9 us (0.905)
  Pallas kernels: 84.4 us -> 78.1 us
  local copies, waits for them, and re-layouts: 3.64 us -> 1.66 us
    pallas_call x1, Pallas kernels: 84.4 us -> 78.1 us  [local(): pl.pallas_call(functools.partial(step_kernel, n_gx, n_gy, n_gz, slots, pi...]
    unnamed x2 -> x3, local copies, waits for them, and re-layouts: 3.03 us -> 1.66 us
where the time goes in v2:
time: 79.9 us; the launch traced here: 79.8 us
  Pallas kernels  78.1 us (98%)
  local copies, waits for them, and re-layouts  1.66 us (2%)
    pallas_call x1, Pallas kernels, local(): pl.pallas_call(functools.partial(step_kernel, n_gx, n_gy, n_gz, slots, pi...  78.1 us
    unnamed x3, local copies, waits for them, and re-layouts  1.66 us

profile of v2, /device:TPU:0, one launch (start us, length us, event | category | flops | bytes accessed | tf_op | source)
XLA Modules:
  0.0 79.8 jit_solution(5302522247522511939)
XLA Ops:
  0.0 0.0 copy-start
  0.0 0.7 copy-done
  0.7 78.1 %purify.1 = f32[32,8192]{1,0:T(8,128)S(1)} custom-call(bf16[192,128,128]{2,1,0:T(8,128)(2,1)} %bitcast.3, s32[1,6,1,32]{3,2,1,0:T(1,128)S(1)} %bitcast.2), custom_call_target="tpu_custom_call" | custom-call | tf_op jit(solution)/shard_map/purify/pallas_call | solution.py:438
  78.8 1.0 %copy.4 = f32[32,8192]{1,0:T(8,128)} copy(f32[32,8192]{1,0:T(8,128)S(1)} %purify.1) | data formatting | bytes 2097152
Async XLA Ops:
  0.0 0.7 copy-start

commit v3 on v2

--- a/solution.py
+++ b/solution.py
@@ -12,6 +12,7 @@
 VMEM = 67043328
 MESH = pl.DeviceIdType.MESH
 HOP_LAG, SIDE_LAG, LAST_LAG = 3, 2, 6
+SEED_HOP, TURN_AT, TURN_LAST, JOIN_LAG, COLLECT_LAG, PASS_LAG, END_LAG = 2, 6, 6, 4, 2, 4, 5
 PIECES = 8
 
 
@@ -21,7 +22,7 @@
             return pieces
 
 
-def greet(axes):
+def greet(axes, plane):
     barrier = pltpu.get_barrier_semaphore()
     total = 0
     for axis in axes:
@@ -32,6 +33,14 @@
                 barrier, inc=1, device_id={axis: lax.rem(me + step, size)}, device_id_type=MESH
             )
         total += size - 1
+    if plane:
+        n_gx, n_gy = lax.axis_size("gx"), lax.axis_size("gy")
+        for dx in range(1, n_gx):
+            for dy in range(1, n_gy):
+                peer = {"gx": lax.rem(lax.axis_index("gx") + dx, n_gx),
+                        "gy": lax.rem(lax.axis_index("gy") + dy, n_gy)}
+                pl.semaphore_signal(barrier, inc=1, device_id=peer, device_id_type=MESH)
+        total += (n_gx - 1) * (n_gy - 1)
     pl.semaphore_wait(barrier, total)
 
 
@@ -43,19 +52,21 @@
 
 
 def step_kernel(
-    n_gx, n_gy, n_gz, slots, pieces, buffers,
+    n_gx, n_gy, n_gz, slots, pieces, buffers, twos,
     tiles, cols, out,
     held, window, current, heads, table_v, lists_v, table, lists,
     own, right_out, left_out, right_in, left_in, square, rounded,
     product, side_out, side_in, mixed, last_out, last_in,
     load_sem, head_sem, head_side, win_send, win_recv, fan_send, fan_recv, table_sem,
     right_send, left_send, right_recv, left_recv, side_send, side_recv, last_send, last_recv, credit,
+    *more,
 ):
     gx, gy, gz = lax.axis_index("gx"), lax.axis_index("gy"), lax.axis_index("gz")
     rows = cols.shape[3]
     size = tiles.shape[2]
     count = n_gx * rows
     chunks = window.shape[0]
+    block = size // n_gy
     high = n_gy * SUB
     wide = rows // pieces
     broad = count // pieces
@@ -73,7 +84,7 @@
             load_sem.at[part + 1],
         ))
         loads[-1].start()
-    greet(("gx", "gy", "gz"))
+    greet(("gx", "gy", "gz"), twos > 0)
 
     def win_copy(m, peer):
         return remote(window.at[m, gx], window.at[m, gx], win_send.at[peer], win_recv.at[m], "gy", peer)
@@ -119,7 +130,7 @@
             tile = held[k].astype(f32)
             for m in range(chunks):
                 window[m, gx, k] = jnp.concatenate(
-                    [tile[q * chunks * SUB + m * SUB:][:SUB] for q in range(n_gy)], axis=0
+                    [tile[q * block + m * SUB:][:SUB] for q in range(n_gy)], axis=0
                 ).astype(bf16)
         for m in range(chunks):
             for peer in range(1, n_gy):
@@ -140,6 +151,56 @@
         lists_v[SUB + i:SUB + i + 1] = jnp.where(top < 0, 0, row * slots + slot)
     list_copy = pltpu.make_async_copy(lists_v, lists, table_sem.at[0])
     list_copy.start()
+    for load in loads[1:]:
+        load.wait()
+
+    @pl.when(gy != 0)
+    def _():
+        first_load.wait()
+
+    list_copy.wait()
+    if twos:
+        (seed, ids, lists2_v, lists2, listed_v, listed_s, product2, mixed2, side2_out, side2_in,
+         last2_out, last2_in, gat, s2_out, s2_in, full, r_out, r_in, z_in,
+         seed_send, seed_recv, ids_send, ids_recv, table2_sem, side2_send, side2_recv, last2_send, last2_recv,
+         gat_send, gat_recv, s2_send, s2_recv, r_send, r_recv, z_send, z_recv) = more
+        tall2 = twos * SUB
+        high2 = n_gy * tall2
+        down2 = pl.ds(block - tall2, tall2)
+        plane = n_gy * n_gx
+        me = gy * n_gx + gx
+        seeds = seed_recv.shape[0]
+        each_seed = slots // seeds
+        listed_v[...] = spread
+        listed_copy = pltpu.make_async_copy(listed_v, listed_s, table2_sem.at[0])
+        listed_copy.start()
+        seed[slots] = jnp.zeros((n_gx, high2, size), bf16)
+
+        def seed_copy(p):
+            part = seed.at[pl.ds(p * each_seed, each_seed)]
+            return remote(part, part, seed_send, seed_recv.at[p], "gz", lax.rem(gz + 1, n_gz))
+
+        def ids_copy(peer):
+            return remote(lists_v.at[pl.ds(0, SUB)], ids, ids_send.at[peer], ids_recv, "gz", peer)
+
+        @pl.when(gz == 0)
+        def _():
+            for peer in range(1, n_gz):
+                ids_copy(peer).start()
+            ids[...] = lists_v[0:SUB]
+            across = lax.broadcasted_iota(jnp.int32, (high2, size), 1)
+            at = lax.broadcasted_iota(jnp.int32, (high2, size), 0)
+            pick = (at // tall2) * block + (block - tall2) + at % tall2
+            pick = jnp.where(across == pick, 1.0, 0.0).astype(bf16)
+            for p in range(seeds):
+                for i in range(p * each_seed, (p + 1) * each_seed):
+                    for g in range(n_gx):
+                        tile = held[lists[SUB + i, g * rows]]
+                        seed[i, g] = lax.dot_general(
+                            pick, tile, (((1,), (1,)), ((), ())), preferred_element_type=f32
+                        ).astype(bf16)
+                seed_copy(p).start()
+
     for g in range(n_gx):
         current[g, slots] = jnp.zeros((high, size), bf16)
     for parity in range(2):
@@ -172,15 +233,23 @@
                 fan_copy(m, d).start()
 
     forward(0)
-    for load in loads[1:]:
-        load.wait()
-
-    @pl.when(gy != 0)
-    def _():
-        first_load.wait()
-
-    list_copy.wait()
     table_copy.wait()
+    if twos:
+        @pl.when(gz > 0)
+        def _():
+            ids_copy(0).wait_recv()
+
+        mine = lists_v[0:SUB]
+        for g in range(n_gx):
+            found = jnp.full((SUB, LANES), slots, jnp.int32)
+            for j in range(slots):
+                label = jnp.broadcast_to(ids[j:j + 1, g * rows:g * rows + 1], (SUB, LANES))
+                found = jnp.where(mine == label, j, found)
+            lists2_v[g * SUB:(g + 1) * SUB] = jnp.where(mine >= rows, slots, found)
+        lists2_copy = pltpu.make_async_copy(lists2_v, lists2, table2_sem.at[1])
+        lists2_copy.start()
+        listed_copy.wait()
+        lists2_copy.wait()
 
     def right_copy(t):
         return remote(right_out.at[t], right_in.at[t], right_send, right_recv.at[t],
@@ -214,9 +283,6 @@
         peer = lax.rem(gy + d, n_gy)
         return remote(last_out.at[v, peer], last_in.at[v, d - 1], last_send, last_recv.at[v],
                       "gy", peer)
-
-    def during(t):
-        return (t >= 0) & (t < steps)
 
     def stage_own(t):
         m, q = t // pieces, lax.rem(t, pieces)
@@ -369,25 +435,182 @@
                 across = pl.ds(pl.multiple_of((q * broad + i + h) * size, size), size)
                 out[down, across] += value[h * SUB:(h + 1) * SUB]
 
+    def pass_seed(p):
+        @pl.when(gz > 0)
+        def _():
+            seed_copy(p).wait_recv()
+
+        @pl.when((gz > 0) & (gz < n_gz - 1))
+        def _():
+            seed_copy(p).start()
+
+    def across_of(c):
+        return pl.ds(pl.multiple_of(c * size, size), size)
+
+    def side2_copy(q, d):
+        peer = lax.rem(gx + d, n_gx)
+        return remote(side2_out.at[q, peer], side2_in.at[q, d - 1], side2_send, side2_recv.at[q], "gx", peer)
+
+    def last2_copy(q, d):
+        peer = lax.rem(gy + d, n_gy)
+        return remote(last2_out.at[q, peer], last2_in.at[q, d - 1], last2_send, last2_recv.at[q], "gy", peer)
+
+    def gat_copy(q, d):
+        return remote(gat.at[q, 0], gat.at[q, d], gat_send, gat_recv.at[q], "gy", lax.rem(gy + d, n_gy))
+
+    def s2_copy(q, d):
+        return remote(s2_out.at[q], s2_in.at[q, d - 1], s2_send, s2_recv.at[q], "gx", lax.rem(gx + d, n_gx))
+
+    def wait_all(ref, send, recv):
+        remote(ref, ref, send, recv, "gy", lax.rem(gy + 1, n_gy)).wait_recv()
+
+    def turn_first(q):
+        hold = lax.rem(q, SIDE_LAG + 1)
+        depth = min(slots, rows)
+        for i in range(broad):
+            c = q * broad + i
+            lhs = jnp.concatenate([
+                jnp.concatenate([seed[lists2[g * SUB + j, c], g] for g in range(n_gx)], axis=0)
+                for j in range(depth)
+            ], axis=1)
+            rhs = jnp.concatenate([held[lists[SUB + j, c]] for j in range(depth)], axis=0)
+            value = jnp.dot(lhs, rhs, preferred_element_type=f32)
+            mine = value[:high2]
+            for g in range(1, n_gx):
+                mine = jnp.where(gx == g, value[g * high2:(g + 1) * high2], mine)
+            product2[hold, i] = mine
+            for g in range(n_gx):
+                side2_out[q, g, i] = value[g * high2:(g + 1) * high2].astype(bf16)
+        for d in range(1, n_gx):
+            side2_copy(q, d).start()
+
+    def turn_mix(q):
+        hold = lax.rem(q, SIDE_LAG + 1)
+        wait_all(side2_in.at[q], side2_send, side2_recv.at[q])
+        for i in range(broad):
+            value = product2[hold, i]
+            for d in range(1, n_gx):
+                value = value + side2_in[q, d - 1, i].astype(f32)
+            mixed2[i] = value
+            for y in range(n_gy):
+                last2_out[q, y, i] = value[y * tall2:(y + 1) * tall2].astype(bf16)
+        for d in range(1, n_gy):
+            last2_copy(q, d).start()
+        for i in range(broad):
+            out[down2, across_of(q * broad + i)] = mixed2[i, pl.ds(pl.multiple_of(gy * tall2, tall2), tall2)]
+
+    def turn_last(q):
+        wait_all(last2_in.at[q], last2_send, last2_recv.at[q])
+        for i in range(broad):
+            total = out[down2, across_of(q * broad + i)]
+            for d in range(1, n_gy):
+                total = total + last2_in[q, d - 1, i].astype(f32)
+            gat[q, 0, i] = total.astype(bf16)
+            out[down2, across_of(q * broad + i)] = 3.0 * total
+        for d in range(1, n_gy):
+            gat_copy(q, d).start()
+
+    def turn_join(q):
+        wait_all(gat.at[q, pl.ds(1, n_gy - 1)], gat_send, gat_recv.at[q])
+        for i in range(broad):
+            tile = jnp.concatenate([gat[q, lax.rem(gy - y + n_gy, n_gy), i] for y in range(n_gy)], axis=0)
+            s2_out[q, i] = tile
+            full[gx, q * broad + i] = tile
+        for d in range(1, n_gx):
+            s2_copy(q, d).start()
+
+    def turn_collect(q):
+        wait_all(s2_in.at[q], s2_send, s2_recv.at[q])
+        for d in range(1, n_gx):
+            g = lax.rem(gx - d + n_gx, n_gx)
+            full[g, pl.ds(q * broad, broad)] = s2_in[q, d - 1]
+
+    def turn_back(q):
+        for i in range(wide):
+            c = q * wide + i
+            lhs = jnp.concatenate([
+                jnp.concatenate([full[g, listed_s[c, j]] for g in range(n_gx)], axis=0)
+                for j in range(slots)
+            ], axis=1)
+            rhs = jnp.concatenate([held[c * slots + j] for j in range(slots)], axis=1)
+            value = -2.0 * lax.dot_general(lhs, rhs, (((1,), (1,)), ((), ())), preferred_element_type=f32)
+            for g in range(n_gx):
+                for y in range(n_gy):
+                    low = g * high2 + y * tall2
+                    r_out[q, y * n_gx + g, i] = value[low:low + tall2].astype(bf16)
+        for d in range(1, plane):
+            peer = lax.rem(me + d, plane)
+            pltpu.make_async_remote_copy(
+                src_ref=r_out.at[q, peer], dst_ref=r_in.at[q, plane - d], send_sem=r_send, recv_sem=r_recv.at[q],
+                device_id={"gx": lax.rem(peer, n_gx), "gy": peer // n_gx}, device_id_type=MESH,
+            ).start()
+        r_in[q, 0] = r_out[q, me]
+
+    def from_slab(a, x):
+        return lax.rem(a * n_gx + x - me + plane, plane)
+
+    def turn_pass(q):
+        wait_all(r_in.at[q, pl.ds(1, plane - 1)], r_send, r_recv.at[q])
+        for d in range(1, n_gz):
+            a = lax.rem(gz + d, n_gz)
+            for x in range(n_gx):
+                remote(r_in.at[q, from_slab(a, x)], z_in.at[q, d - 1, x], z_send, z_recv.at[q], "gz", a).start()
+
+    def turn_end(q):
+        wait_all(z_in.at[q], z_send, z_recv.at[q])
+        for x in range(n_gx):
+            for i in range(wide):
+                value = r_in[q, from_slab(gz, x), i].astype(f32)
+                for d in range(1, n_gz):
+                    value = value + z_in[q, d - 1, x, i].astype(f32)
+                out[down2, across_of(x * rows + q * wide + i)] += value
+
     sum_at = (n_gz - 1) * HOP_LAG
     second_at = sum_at + pieces
     mix_at = second_at + SIDE_LAG
     last_at = mix_at + LAST_LAG
 
+    stages = [
+        (stage_own, 0, steps),
+        (stage_right, gz * HOP_LAG, steps),
+        (stage_left, (n_gz - 1 - gz) * HOP_LAG, steps),
+        (stage_sum, sum_at, steps),
+        (stage_mix, mix_at, steps),
+        (stage_second, second_at, steps),
+        (stage_last, last_at, steps),
+    ]
+    slots_needed = steps + last_at
+    if twos:
+        turn_mix_at = TURN_AT + SIDE_LAG
+        turn_last_at = turn_mix_at + TURN_LAST
+        join_at = turn_last_at + JOIN_LAG
+        collect_at = join_at + COLLECT_LAG
+        back_at = collect_at + pieces
+        pass_at = back_at + PASS_LAG
+        end_at = pass_at + END_LAG
+        stages = stages[:4] + [
+            (pass_seed, (gz - 1) * SEED_HOP, seeds),
+            (stage_mix, mix_at, steps),
+            (turn_mix, turn_mix_at, pieces),
+            (turn_pass, pass_at, pieces),
+            (turn_back, back_at, pieces),
+            (stage_second, second_at, steps),
+            (turn_first, TURN_AT, pieces),
+            (stage_last, last_at, steps),
+            (turn_last, turn_last_at, pieces),
+            (turn_join, join_at, pieces),
+            (turn_collect, collect_at, pieces),
+            (turn_end, end_at, pieces),
+        ]
+        slots_needed = max(slots_needed, end_at + pieces)
+
     def slot(s, carry):
-        for stage, delay in (
-            (stage_own, 0),
-            (stage_right, gz * HOP_LAG),
-            (stage_left, (n_gz - 1 - gz) * HOP_LAG),
-            (stage_sum, sum_at),
-            (stage_mix, mix_at),
-            (stage_second, second_at),
-            (stage_last, last_at),
-        ):
-            pl.when(during(s - delay))(functools.partial(stage, s - delay))
+        for stage, delay, span in stages:
+            t = s - delay
+            pl.when((t >= 0) & (t < span))(functools.partial(stage, t))
         return carry
 
-    lax.fori_loop(0, steps + last_at, slot, jnp.int32(0))
+    lax.fori_loop(0, slots_needed, slot, jnp.int32(0))
 
     @pl.when(gz < n_gz - 1)
     def _():
@@ -405,6 +628,26 @@
         def _(t):
             side_all(t).wait_send()
 
+    if twos:
+        def sent(ref, send, recv):
+            remote(ref, ref, send, recv, "gy", lax.rem(gy + 1, n_gy)).wait_send()
+
+        sent(side2_in, side2_send, side2_recv.at[0])
+        sent(last2_in, last2_send, last2_recv.at[0])
+        sent(gat.at[:, pl.ds(1, n_gy - 1)], gat_send, gat_recv.at[0])
+        sent(s2_in, s2_send, s2_recv.at[0])
+        sent(r_in.at[:, pl.ds(1, plane - 1)], r_send, r_recv.at[0])
+        sent(z_in, z_send, z_recv.at[0])
+
+        @pl.when(gz < n_gz - 1)
+        def _():
+            sent(seed.at[pl.ds(0, slots)], seed_send, seed_recv.at[0])
+
+        @pl.when(gz == 0)
+        def _():
+            for peer in range(1, n_gz):
+                ids_copy(peer).wait_send()
+
     for d in range(1, n_gx):
         head_fan(d).wait_send()
         whole = window.at[:, gx]
@@ -425,6 +668,8 @@
     tiles = block_values.reshape(rows * slots, size, size)
     count = n_gx * rows
     chunks = size // (n_gy * SUB)
+    twos = 1 if n_gx <= 4 and chunks > 2 and n_gy == n_gz else 0
+    chunks = chunks - twos
     high = n_gy * SUB
     pieces = pieces_of(rows, PIECES)
     wide, broad, steps = rows // pieces, count // pieces, chunks * pieces
@@ -435,8 +680,36 @@
     dma = pltpu.SemaphoreType.DMA
     f32, bf16 = jnp.float32, jnp.bfloat16
     flow = (steps, wide, tall, size)
+    more = []
+    if twos:
+        tall2 = twos * SUB
+        high2, plane, seeds = n_gy * tall2, n_gy * n_gx, pieces_of(slots, 3)
+        more = [
+            pltpu.VMEM((slots + 1, n_gx, high2, size), bf16),
+            pltpu.VMEM((SUB, LANES), jnp.int32),
+            pltpu.VMEM((n_gx * SUB, LANES), jnp.int32),
+            pltpu.SMEM((n_gx * SUB, LANES), jnp.int32),
+            pltpu.VMEM((rows, LANES), jnp.int32),
+            pltpu.SMEM((rows, LANES), jnp.int32),
+            pltpu.VMEM((SIDE_LAG + 1, broad, high2, size), f32),
+            pltpu.VMEM((broad, high2, size), f32),
+            pltpu.VMEM((pieces, n_gx, broad, high2, size), bf16),
+            pltpu.VMEM((pieces, n_gx - 1, broad, high2, size), bf16),
+            pltpu.VMEM((pieces, n_gy, broad, tall2, size), bf16),
+            pltpu.VMEM((pieces, n_gy - 1, broad, tall2, size), bf16),
+            pltpu.VMEM((pieces, n_gy, broad, tall2, size), bf16),
+            pltpu.VMEM((pieces, broad, high2, size), bf16),
+            pltpu.VMEM((pieces, n_gx - 1, broad, high2, size), bf16),
+            pltpu.VMEM((n_gx, count, high2, size), bf16),
+            pltpu.VMEM((pieces, plane, wide, tall2, size), bf16),
+            pltpu.VMEM((pieces, plane, wide, tall2, size), bf16),
+            pltpu.VMEM((pieces, n_gz - 1, n_gx, wide, tall2, size), bf16),
+            dma, dma((seeds,)), dma((n_gz,)), dma, dma((2,)),
+            dma, dma((pieces,)), dma, dma((pieces,)), dma, dma((pieces,)),
+            dma, dma((pieces,)), dma, dma((pieces,)), dma, dma((pieces,)),
+        ]
     return pl.pallas_call(
-        functools.partial(step_kernel, n_gx, n_gy, n_gz, slots, pieces, buffers),
+        functools.partial(step_kernel, n_gx, n_gy, n_gz, slots, pieces, buffers, twos),
         out_shape=jax.ShapeDtypeStruct((size // n_gy, count * size), f32),
         in_specs=[pl.BlockSpec(memory_space=pl.ANY), pl.BlockSpec(memory_space=pltpu.VMEM)],
         out_specs=pl.BlockSpec(memory_space=pltpu.VMEM),
@@ -465,7 +738,7 @@
             dma((1 if buffers == chunks else buffers * pieces,)), dma((buffers * pieces,)),
             dma, dma((steps,)),
             pltpu.SemaphoreType.REGULAR,
-        ],
+        ] + more,
         compiler_params=pltpu.CompilerParams(
             collective_id=0, has_side_effects=True, vmem_limit_bytes=limit
         ),

time: 79.9 us -> 72.7 us (0.910)
  Pallas kernels: 78.1 us -> 70.9 us
    pallas_call x1, Pallas kernels: 78.1 us -> 70.9 us  [local(): pl.pallas_call(functools.partial(step_kernel, n_gx, n_gy, n_gz, slots, pi...]
where the time goes in v3:
time: 72.7 us; the launch traced here: 72.6 us
  Pallas kernels  70.9 us (98%)
  local copies, waits for them, and re-layouts  1.66 us (2%)
    pallas_call x1, Pallas kernels, local(): pl.pallas_call(functools.partial(step_kernel, n_gx, n_gy, n_gz, slots, pi...  70.9 us
    unnamed x3, local copies, waits for them, and re-layouts  1.66 us

profile of v3, /device:TPU:0, one launch (start us, length us, event | category | flops | bytes accessed | tf_op | source)
XLA Modules:
  0.0 72.6 jit_solution(2288432182557731797)
XLA Ops:
  0.0 0.0 copy-start
  0.0 0.7 copy-done
  0.7 70.9 %purify.1 = f32[32,8192]{1,0:T(8,128)S(1)} custom-call(bf16[192,128,128]{2,1,0:T(8,128)(2,1)} %bitcast.3, s32[1,6,1,32]{3,2,1,0:T(1,128)S(1)} %bitcast.2), custom_call_target="tpu_custom_call" | custom-call | tf_op jit(solution)/shard_map/purify/pallas_call | solution.py:711
  71.6 1.0 %copy.4 = f32[32,8192]{1,0:T(8,128)} copy(f32[32,8192]{1,0:T(8,128)S(1)} %purify.1) | data formatting | bytes 2097152
Async XLA Ops:
  0.0 0.7 copy-start

commit v4 on v3

--- a/solution.py
+++ b/solution.py
@@ -11,9 +11,9 @@
 SUB = 8
 VMEM = 67043328
 MESH = pl.DeviceIdType.MESH
-HOP_LAG, SIDE_LAG, LAST_LAG = 3, 2, 6
-SEED_HOP, TURN_AT, TURN_LAST, JOIN_LAG, COLLECT_LAG, PASS_LAG, END_LAG = 2, 6, 6, 4, 2, 4, 5
-PIECES = 8
+HOP_LAG, SIDE_LAG, LAST_LAG = 6, 2, 6
+SEED_HOP, TURN_AT, TURN_LAST, JOIN_LAG, COLLECT_LAG, PASS_LAG, END_LAG = 2, 6, 6, 4, 2, 5, 7
+PIECES, GROUPS = 8, 4
 
 
 def pieces_of(count, most):
@@ -22,7 +22,7 @@
             return pieces
 
 
-def greet(axes, plane):
+def knock(axes, plane):
     barrier = pltpu.get_barrier_semaphore()
     total = 0
     for axis in axes:
@@ -41,7 +41,7 @@
                         "gy": lax.rem(lax.axis_index("gy") + dy, n_gy)}
                 pl.semaphore_signal(barrier, inc=1, device_id=peer, device_id_type=MESH)
         total += (n_gx - 1) * (n_gy - 1)
-    pl.semaphore_wait(barrier, total)
+    return lambda: pl.semaphore_wait(barrier, total)
 
 
 def remote(src, dst, send, recv, axis, peer):
@@ -84,7 +84,7 @@
             load_sem.at[part + 1],
         ))
         loads[-1].start()
-    greet(("gx", "gy", "gz"), twos > 0)
+    enter = knock(("gx", "gy", "gz"), twos > 0)
 
     def win_copy(m, peer):
         return remote(window.at[m, gx], window.at[m, gx], win_send.at[peer], win_recv.at[m], "gy", peer)
@@ -121,10 +121,6 @@
     @pl.when(gy == 0)
     def _():
         heads[gx] = spread[:heads.shape[1]]
-        for peer in range(1, n_gy):
-            head_copy(peer).start()
-        for d in range(1, n_gx):
-            head_fan(d).start()
         first_load.wait()
         for k in range(slots):
             tile = held[k].astype(f32)
@@ -132,11 +128,6 @@
                 window[m, gx, k] = jnp.concatenate(
                     [tile[q * block + m * SUB:][:SUB] for q in range(n_gy)], axis=0
                 ).astype(bf16)
-        for m in range(chunks):
-            for peer in range(1, n_gy):
-                win_copy(m, peer).start()
-            for d in range(1, n_gx):
-                fan_copy(m, d).start()
 
     marks = [jnp.where(each[k] == lanes, places * SUB + k, -1) for k in range(slots)]
     lists_v[...] = jnp.zeros_like(lists_v)
@@ -151,6 +142,20 @@
         lists_v[SUB + i:SUB + i + 1] = jnp.where(top < 0, 0, row * slots + slot)
     list_copy = pltpu.make_async_copy(lists_v, lists, table_sem.at[0])
     list_copy.start()
+    enter()
+
+    @pl.when(gy == 0)
+    def _():
+        for peer in range(1, n_gy):
+            head_copy(peer).start()
+        for d in range(1, n_gx):
+            head_fan(d).start()
+        for m in range(chunks):
+            for peer in range(1, n_gy):
+                win_copy(m, peer).start()
+            for d in range(1, n_gx):
+                fan_copy(m, d).start()
+
     for load in loads[1:]:
         load.wait()
 
@@ -171,6 +176,7 @@
         me = gy * n_gx + gx
         seeds = seed_recv.shape[0]
         each_seed = slots // seeds
+        per = pieces // r_recv.shape[0]
         listed_v[...] = spread
         listed_copy = pltpu.make_async_copy(listed_v, listed_s, table2_sem.at[0])
         listed_copy.start()
@@ -202,7 +208,8 @@
                 seed_copy(p).start()
 
     for g in range(n_gx):
-        current[g, slots] = jnp.zeros((high, size), bf16)
+        for m in range(chunks):
+            current[m, g, slots] = jnp.zeros((high, size), bf16)
     for parity in range(2):
         rounded[parity, rows] = jnp.zeros((n_gx * high, size), bf16)
 
@@ -284,29 +291,40 @@
         return remote(last_out.at[v, peer], last_in.at[v, d - 1], last_send, last_recv.at[v],
                       "gy", peer)
 
-    def stage_own(t):
-        m, q = t // pieces, lax.rem(t, pieces)
-
-        @pl.when((q == 1 % pieces) & (m + 1 < chunks))
-        def _():
-            forward(m + 1)
-
-        @pl.when(q == 0)
-        def _():
-            for d in range(1, n_gx):
-                fan_landing(m, d).wait_recv()
-            for g in range(n_gx):
-                for k in range(slots):
-                    current[g, k] = window[m, g, k]
-
+    def fetch(m):
+        for d in range(1, n_gx):
+            fan_landing(m, d).wait_recv()
+        for g in range(n_gx):
+            for k in range(slots):
+                current[m, g, k] = window[m, g, k]
+
+    def multiply(q, ms):
         for i in range(wide):
             c = q * wide + i
             lhs = jnp.concatenate([
-                jnp.concatenate([current[g, table[c, g * SUB + j]] for g in range(n_gx)], axis=0)
+                jnp.concatenate([current[m, g, table[c, g * SUB + j]] for m in ms for g in range(n_gx)], axis=0)
                 for j in range(slots)
             ], axis=1)
             rhs = jnp.concatenate([held[c * slots + j] for j in range(slots)], axis=1)
-            own[t, i] = lax.dot_general(lhs, rhs, (((1,), (1,)), ((), ())), preferred_element_type=f32)
+            value = lax.dot_general(lhs, rhs, (((1,), (1,)), ((), ())), preferred_element_type=f32)
+            for n, m in enumerate(ms):
+                own[m * pieces + q, i] = value[n * n_gx * high:(n + 1) * n_gx * high]
+
+    def stage_own(t):
+        @pl.when((t > 0) & (t < chunks))
+        def _():
+            forward(t)
+
+        spans = [[0], list(range(1, chunks))] if twos else [[m] for m in range(chunks)]
+        for n, ms in enumerate(spans):
+            @pl.when(t == n * pieces)
+            def _():
+                for m in ms:
+                    fetch(m)
+
+            @pl.when((t >= n * pieces) & (t < (n + 1) * pieces))
+            def _():
+                multiply(t - n * pieces, ms)
 
     def stage_right(t):
         @pl.when(gz == 0)
@@ -407,11 +425,15 @@
                 mixed[h] = value
                 pair.append(value)
             for y in range(n_gy):
-                last_out[v, y, i // 2] = jnp.concatenate(
+                last_out[v // 2, y, lax.rem(v, 2), i // 2] = jnp.concatenate(
                     [value[y * SUB:(y + 1) * SUB] for value in pair], axis=0
                 ).astype(bf16)
-        for d in range(1, n_gy):
-            last_copy(v, d).start()
+
+        @pl.when(lax.rem(v, 2) == 1)
+        def _():
+            for d in range(1, n_gy):
+                last_copy(v // 2, d).start()
+
         if buffers < chunks:
             @pl.when((q == pieces - 1) & (m + buffers < chunks))
             def _():
@@ -425,15 +447,19 @@
 
     def stage_last(w):
         m, q = w // pieces, lax.rem(w, pieces)
-        last_all(w).wait_recv()
         down = pl.ds(pl.multiple_of(m * SUB, SUB), SUB)
-        for i in range(0, broad, 2):
-            value = last_in[w, 0, i // 2].astype(f32)
-            for d in range(2, n_gy):
-                value = value + last_in[w, d - 1, i // 2].astype(f32)
-            for h in range(2):
-                across = pl.ds(pl.multiple_of((q * broad + i + h) * size, size), size)
-                out[down, across] += value[h * SUB:(h + 1) * SUB]
+
+        @pl.when(lax.rem(w, 2) == 1)
+        def _():
+            last_all(w // 2).wait_recv()
+            for n in range(2):
+                for i in range(0, broad, 2):
+                    value = last_in[w // 2, 0, n, i // 2].astype(f32)
+                    for d in range(2, n_gy):
+                        value = value + last_in[w // 2, d - 1, n, i // 2].astype(f32)
+                    for h in range(2):
+                        across = pl.ds(pl.multiple_of(((q - 1 + n) * broad + i + h) * size, size), size)
+                        out[down, across] += value[h * SUB:(h + 1) * SUB]
 
     def pass_seed(p):
         @pl.when(gz > 0)
@@ -526,6 +552,7 @@
             full[g, pl.ds(q * broad, broad)] = s2_in[q, d - 1]
 
     def turn_back(q):
+        group = q // per
         for i in range(wide):
             c = q * wide + i
             lhs = jnp.concatenate([
@@ -537,43 +564,63 @@
             for g in range(n_gx):
                 for y in range(n_gy):
                     low = g * high2 + y * tall2
-                    r_out[q, y * n_gx + g, i] = value[low:low + tall2].astype(bf16)
-        for d in range(1, plane):
-            peer = lax.rem(me + d, plane)
-            pltpu.make_async_remote_copy(
-                src_ref=r_out.at[q, peer], dst_ref=r_in.at[q, plane - d], send_sem=r_send, recv_sem=r_recv.at[q],
-                device_id={"gx": lax.rem(peer, n_gx), "gy": peer // n_gx}, device_id_type=MESH,
-            ).start()
-        r_in[q, 0] = r_out[q, me]
+                    r_out[group, y * n_gx + g, lax.rem(q, per) * wide + i] = value[low:low + tall2].astype(bf16)
+
+        @pl.when(lax.rem(q, per) == per - 1)
+        def _():
+            for d in range(1, plane):
+                peer = lax.rem(me + d, plane)
+                pltpu.make_async_remote_copy(
+                    src_ref=r_out.at[group, peer], dst_ref=r_in.at[group, plane - d],
+                    send_sem=r_send, recv_sem=r_recv.at[group],
+                    device_id={"gx": lax.rem(peer, n_gx), "gy": peer // n_gx}, device_id_type=MESH,
+                ).start()
+            r_in[group, 0] = r_out[group, me]
 
     def from_slab(a, x):
         return lax.rem(a * n_gx + x - me + plane, plane)
 
     def turn_pass(q):
-        wait_all(r_in.at[q, pl.ds(1, plane - 1)], r_send, r_recv.at[q])
-        for d in range(1, n_gz):
-            a = lax.rem(gz + d, n_gz)
-            for x in range(n_gx):
-                remote(r_in.at[q, from_slab(a, x)], z_in.at[q, d - 1, x], z_send, z_recv.at[q], "gz", a).start()
+        group = q // per
+
+        @pl.when(lax.rem(q, per) == per - 1)
+        def _():
+            wait_all(r_in.at[group, pl.ds(1, plane - 1)], r_send, r_recv.at[group])
+            for d in range(1, n_gz):
+                a = lax.rem(gz + d, n_gz)
+                for x in range(n_gx):
+                    remote(r_in.at[group, from_slab(a, x)], z_in.at[group, d - 1, x],
+                           z_send, z_recv.at[group], "gz", a).start()
 
     def turn_end(q):
-        wait_all(z_in.at[q], z_send, z_recv.at[q])
+        group = q // per
+
+        @pl.when(lax.rem(q, per) == 0)
+        def _():
+            wait_all(z_in.at[group], z_send, z_recv.at[group])
+
         for x in range(n_gx):
             for i in range(wide):
-                value = r_in[q, from_slab(gz, x), i].astype(f32)
+                n = lax.rem(q, per) * wide + i
+                value = r_in[group, from_slab(gz, x), n].astype(f32)
                 for d in range(1, n_gz):
-                    value = value + z_in[q, d - 1, x, i].astype(f32)
+                    value = value + z_in[group, d - 1, x, n].astype(f32)
                 out[down2, across_of(x * rows + q * wide + i)] += value
 
-    sum_at = (n_gz - 1) * HOP_LAG
-    second_at = sum_at + pieces
+    def hops(count, extra):
+        return count * (HOP_LAG // 2) + (count + extra) // 2 * (HOP_LAG % 2)
+
+    behind, ahead = gz, n_gz - 1 - gz
+    right_at, left_at = hops(behind, 0), hops(ahead, n_gz % 2 + 1)
+    sum_at = max(hops(n_gz - 1, 0), hops(n_gz - 1, n_gz % 2 + 1))
+    second_at = sum_at + pieces - 1
     mix_at = second_at + SIDE_LAG
     last_at = mix_at + LAST_LAG
 
     stages = [
         (stage_own, 0, steps),
-        (stage_right, gz * HOP_LAG, steps),
-        (stage_left, (n_gz - 1 - gz) * HOP_LAG, steps),
+        (stage_right, right_at, steps),
+        (stage_left, left_at, steps),
         (stage_sum, sum_at, steps),
         (stage_mix, mix_at, steps),
         (stage_second, second_at, steps),
@@ -585,13 +632,14 @@
         turn_last_at = turn_mix_at + TURN_LAST
         join_at = turn_last_at + JOIN_LAG
         collect_at = join_at + COLLECT_LAG
-        back_at = collect_at + pieces
+        back_at = collect_at + pieces - 1
         pass_at = back_at + PASS_LAG
         end_at = pass_at + END_LAG
         stages = stages[:4] + [
             (pass_seed, (gz - 1) * SEED_HOP, seeds),
             (stage_mix, mix_at, steps),
             (turn_mix, turn_mix_at, pieces),
+            (turn_collect, collect_at, pieces),
             (turn_pass, pass_at, pieces),
             (turn_back, back_at, pieces),
             (stage_second, second_at, steps),
@@ -599,7 +647,6 @@
             (stage_last, last_at, steps),
             (turn_last, turn_last_at, pieces),
             (turn_join, join_at, pieces),
-            (turn_collect, collect_at, pieces),
             (turn_end, end_at, pieces),
         ]
         slots_needed = max(slots_needed, end_at + pieces)
@@ -684,6 +731,7 @@
     if twos:
         tall2 = twos * SUB
         high2, plane, seeds = n_gy * tall2, n_gy * n_gx, pieces_of(slots, 3)
+        groups = pieces_of(pieces, GROUPS)
         more = [
             pltpu.VMEM((slots + 1, n_gx, high2, size), bf16),
             pltpu.VMEM((SUB, LANES), jnp.int32),
@@ -701,12 +749,12 @@
             pltpu.VMEM((pieces, broad, high2, size), bf16),
             pltpu.VMEM((pieces, n_gx - 1, broad, high2, size), bf16),
             pltpu.VMEM((n_gx, count, high2, size), bf16),
-            pltpu.VMEM((pieces, plane, wide, tall2, size), bf16),
-            pltpu.VMEM((pieces, plane, wide, tall2, size), bf16),
-            pltpu.VMEM((pieces, n_gz - 1, n_gx, wide, tall2, size), bf16),
+            pltpu.VMEM((groups, plane, rows // groups, tall2, size), bf16),
+            pltpu.VMEM((groups, plane, rows // groups, tall2, size), bf16),
+            pltpu.VMEM((groups, n_gz - 1, n_gx, rows // groups, tall2, size), bf16),
             dma, dma((seeds,)), dma((n_gz,)), dma, dma((2,)),
             dma, dma((pieces,)), dma, dma((pieces,)), dma, dma((pieces,)),
-            dma, dma((pieces,)), dma, dma((pieces,)), dma, dma((pieces,)),
+            dma, dma((pieces,)), dma, dma((groups,)), dma, dma((groups,)),
         ]
     return pl.pallas_call(
         functools.partial(step_kernel, n_gx, n_gy, n_gz, slots, pieces, buffers, twos),
@@ -716,7 +764,7 @@
         scratch_shapes=[
             pltpu.VMEM((rows * slots, size, size), bf16),
             pltpu.VMEM((chunks, n_gx, slots, high, size), bf16),
-            pltpu.VMEM((n_gx, slots + 1, high, size), bf16),
+            pltpu.VMEM((chunks, n_gx, slots + 1, high, size), bf16),
             pltpu.VMEM((n_gx, top, LANES), jnp.int32),
             pltpu.VMEM((rows, LANES), jnp.int32),
             pltpu.VMEM((2 * SUB, LANES), jnp.int32),
@@ -730,13 +778,13 @@
             pltpu.VMEM((buffers * pieces, n_gx, broad, high, size), bf16),
             pltpu.VMEM((buffers * pieces, n_gx - 1, broad, high, size), bf16),
             pltpu.VMEM((broad, high, size), f32),
-            pltpu.VMEM((steps, n_gy, broad // 2, 2 * SUB, size), bf16),
-            pltpu.VMEM((steps, n_gy - 1, broad // 2, 2 * SUB, size), bf16),
+            pltpu.VMEM((steps // 2, n_gy, 2, broad // 2, 2 * SUB, size), bf16),
+            pltpu.VMEM((steps // 2, n_gy - 1, 2, broad // 2, 2 * SUB, size), bf16),
             dma((1 + min(4, rows - 1),)), dma((2, n_gy)), dma((2, n_gx - 1)),
             dma((n_gy,)), dma((chunks,)), dma((n_gx - 1,)), dma((chunks, n_gx - 1)), dma((2,)),
             dma, dma, dma((steps,)), dma((steps,)),
             dma((1 if buffers == chunks else buffers * pieces,)), dma((buffers * pieces,)),
-            dma, dma((steps,)),
+            dma, dma((steps // 2,)),
             pltpu.SemaphoreType.REGULAR,
         ] + more,
         compiler_params=pltpu.CompilerParams(

time: 72.7 us -> 71.5 us (0.983)
  Pallas kernels: 70.9 us -> 69.6 us
    pallas_call x1, Pallas kernels: 70.9 us -> 69.6 us  [local(): pl.pallas_call(functools.partial(step_kernel, n_gx, n_gy, n_gz, slots, pi...]
where the time goes in v4:
time: 71.5 us; the launch traced here: 71.3 us
  Pallas kernels  69.6 us (97%)
  local copies, waits for them, and re-layouts  1.66 us (2%)
    pallas_call x1, Pallas kernels, local(): pl.pallas_call(functools.partial(step_kernel, n_gx, n_gy, n_gz, slots, pi...  69.6 us
    unnamed x3, local copies, waits for them, and re-layouts  1.66 us

profile of v4, /device:TPU:0, one launch (start us, length us, event | category | flops | bytes accessed | tf_op | source)
XLA Modules:
  0.0 71.3 jit_solution(11769548321178221285)
XLA Ops:
  0.0 0.0 copy-start
  0.0 0.7 copy-done
  0.7 69.6 %purify.1 = f32[32,8192]{1,0:T(8,128)S(1)} custom-call(bf16[192,128,128]{2,1,0:T(8,128)(2,1)} %bitcast.3, s32[1,6,1,32]{3,2,1,0:T(1,128)S(1)} %bitcast.2), custom_call_target="tpu_custom_call" | custom-call | tf_op jit(solution)/shard_map/purify/pallas_call | solution.py:759
  70.3 1.0 %copy.4 = f32[32,8192]{1,0:T(8,128)} copy(f32[32,8192]{1,0:T(8,128)S(1)} %purify.1) | data formatting | bytes 2097152
Async XLA Ops:
  0.0 0.7 copy-start

commit v5 on v4

--- a/solution.py
+++ b/solution.py
@@ -612,7 +612,8 @@
 
     behind, ahead = gz, n_gz - 1 - gz
     right_at, left_at = hops(behind, 0), hops(ahead, n_gz % 2 + 1)
-    sum_at = max(hops(n_gz - 1, 0), hops(n_gz - 1, n_gz % 2 + 1))
+    farthest = max(hops(n_gz - 1, 0), hops(n_gz - 1, n_gz % 2 + 1))
+    sum_at = jnp.maximum(right_at, left_at)
     second_at = sum_at + pieces - 1
     mix_at = second_at + SIDE_LAG
     last_at = mix_at + LAST_LAG
@@ -626,7 +627,7 @@
         (stage_second, second_at, steps),
         (stage_last, last_at, steps),
     ]
-    slots_needed = steps + last_at
+    slots_needed = steps + farthest + pieces - 1 + SIDE_LAG + LAST_LAG
     if twos:
         turn_mix_at = TURN_AT + SIDE_LAG
         turn_last_at = turn_mix_at + TURN_LAST

time: 71.5 us -> 71.7 us (level)
  no operation moved by 1% of the time
where the time goes in v5:
time: 71.7 us; the launch traced here: 71.6 us
  Pallas kernels  69.9 us (97%)
  local copies, waits for them, and re-layouts  1.66 us (2%)
    pallas_call x1, Pallas kernels, local(): pl.pallas_call(functools.partial(step_kernel, n_gx, n_gy, n_gz, slots, pi...  69.9 us
    unnamed x3, local copies, waits for them, and re-layouts  1.66 us

profile of v5, /device:TPU:0, one launch (start us, length us, event | category | flops | bytes accessed | tf_op | source)
XLA Modules:
  0.0 71.6 jit_solution(18189774533851434578)
XLA Ops:
  0.0 0.0 copy-start
  0.0 0.7 copy-done
  0.7 69.9 %purify.1 = f32[32,8192]{1,0:T(8,128)S(1)} custom-call(bf16[192,128,128]{2,1,0:T(8,128)(2,1)} %bitcast.3, s32[1,6,1,32]{3,2,1,0:T(1,128)S(1)} %bitcast.2), custom_call_target="tpu_custom_call" | custom-call | tf_op jit(solution)/shard_map/purify/pallas_call | solution.py:760
  70.6 1.0 %copy.4 = f32[32,8192]{1,0:T(8,128)} copy(f32[32,8192]{1,0:T(8,128)S(1)} %purify.1) | data formatting | bytes 2097152
Async XLA Ops:
  0.0 0.7 copy-start
